TPU v7x, 32 devices: a whole 2x2x4 slice. The times are simulated.
32 devices in a mesh: dp: 8 (over z, x), tensor: 4 (over y, core).
Axes of the slice: x: 2, y: 2, z: 4, core: 2. Of those that a mesh axis runs over, the one named last changes fastest.
Arguments:
- inputs: bfloat16 [4096, 2048], P(('dp', 'tensor')), may hold values from -6 to 6
- cotangent: bfloat16 [4096, 2048], P(('dp', 'tensor')), may hold values from -6 to 6
- log_decay: float32 [8, 4096], P('tensor', 'dp'), may hold values from -1 to 0, as said below
- query_weight: bfloat16 [2048, 2048], P('dp', 'tensor'), may hold values from -0.125 to 0.125
- key_weight: bfloat16 [2048, 2048], P('dp', 'tensor'), may hold values from -0.125 to 0.125
- value_weight: bfloat16 [2048, 4096], P('dp', 'tensor'), may hold values from -0.125 to 0.125
- gate_weight: bfloat16 [2048, 4096], P('dp', 'tensor'), may hold values from -0.125 to 0.125
- out_weight: bfloat16 [4096, 2048], P('tensor', 'dp'), may hold values from -0.09375 to 0.09375
- group_gain: bfloat16 [8, 512], P('tensor', 'dp'), may hold values from 0.25 to 1.75
- norm_gains: bfloat16 [2, 2048], P(None, 'dp'), may hold values from 0.25 to 1.75
- norm_biases: bfloat16 [2, 2048], P(None, 'dp'), may hold values from -1.5 to 1.5
- ffn_gate_weight: bfloat16 [2048, 4096], P('dp', 'tensor'), may hold values from -0.125 to 0.125
- ffn_up_weight: bfloat16 [2048, 4096], P('dp', 'tensor'), may hold values from -0.125 to 0.125
- ffn_down_weight: bfloat16 [4096, 2048], P('tensor', 'dp'), may hold values from -0.09375 to 0.09375
Outputs:
- layer_out: bfloat16 [4096, 2048], P(('dp', 'tensor'))
- input_grad: bfloat16 [4096, 2048], P(('dp', 'tensor'))
- query_grad: float32 [2048, 2048], P('dp', 'tensor')
- key_grad: float32 [2048, 2048], P('dp', 'tensor')
- value_grad: float32 [2048, 4096], P('dp', 'tensor')
- gate_grad: float32 [2048, 4096], P('dp', 'tensor')
- out_weight_grad: float32 [4096, 2048], P('tensor', 'dp')
- group_gain_grad: float32 [8, 512], P('tensor', 'dp')
- norm_gain_grad: float32 [2, 2048], P(None, ('dp', 'tensor'))
- norm_bias_grad: float32 [2, 2048], P(None, ('dp', 'tensor'))
- ffn_gate_grad: float32 [2048, 4096], P('dp', 'tensor')
- ffn_up_grad: float32 [2048, 4096], P('dp', 'tensor')
- ffn_down_grad: float32 [4096, 2048], P('tensor', 'dp')
Inputs may be any that keep to these rules, and one draw needn't show every extreme that they name: `log_decay`: every entry is negative: a per-position log-decay of its head.
All inputs are finite; a program needn't handle non-finite values.
Results may differ from a plain program's by a relative error of at most 0.022.
Values may be sent and summed in bfloat16 or wider, within the bound.
A program may use at most 192 MiB of HBM per device.

v0:
```python
import functools
import math

import jax
import jax.numpy as jnp
from jax import lax
from jax.experimental import pallas as pl
from jax.experimental.pallas import tpu as pltpu
from jax.sharding import PartitionSpec as P

EPSILON = 1e-05
GROUP_FLOOR = 1.0
BF = jnp.bfloat16
F32 = jnp.float32
PAIR = 2
MESH = pl.DeviceIdType.MESH
QK, V, G, O, FG, FU, FD = range(7)
GROUPS = 7


def dot_nn(a, b):
    return lax.dot_general(a, b, (((1,), (0,)), ((), ())), preferred_element_type=F32)


def dot_nt(a, b):
    return lax.dot_general(a, b, (((1,), (1,)), ((), ())), preferred_element_type=F32)


def dot_tn(a, b):
    return lax.dot_general(a, b, (((0,), (0,)), ((), ())), preferred_element_type=F32)


def flip(index, bit):
    return index + bit - 2 * bit * ((index // bit) % 2)


class Place:
    def __init__(self, n_dp):
        self.n_dp = n_dp
        self.d = lax.axis_index("dp")
        self.t = lax.axis_index("tensor")
        self.z = (self.d // PAIR) % 2
        self.rest = [1 << i for i in range(2, n_dp.bit_length() - 1)] + [1]
        self.inner = self.rest[:-1]
        self.masks = []
        for pick in range(1, 1 << (1 + len(self.inner))):
            bits = [PAIR] * (pick & 1) + [b for k, b in enumerate(self.inner) if (pick >> (k + 1)) & 1]
            self.masks.append((bits, pick & ~1, pick & 1))
        half = n_dp // 2
        self.pairs = self.masks + [([1], half, 0)] + [(bits + [1], above + half, flips) for bits, above, flips in self.masks]

    def slot(self, above, flips):
        return next((j for j, pair in enumerate(self.pairs) if pair[1:] == (above, flips)), None)

    def dp_of(self, p):
        out = (p & 1) * PAIR
        for k, bit in enumerate(self.rest):
            here = (self.d // bit) % 2
            out = out + (1 - here if (p >> (k + 1)) & 1 else here) * bit
        return out

    def peer(self, bits):
        out = self.d
        for bit in bits:
            out = flip(out, bit)
        return {"dp": out}

    def x_peer(self):
        return {"dp": flip(self.d, 1)}

    def z_peer(self):
        return {"dp": flip(self.d, PAIR)}

    def y_peer(self):
        return {"tensor": flip(self.t, 2)}

    def c_peer(self):
        return {"tensor": flip(self.t, 1)}

    def everyone(self, far):
        near = [self.x_peer(), self.y_peer(), self.c_peer()]
        if far:
            return near[1:] + [self.peer(bits) for bits, _, _ in self.pairs]
        return near + [self.peer(bits) for bits, _, _ in self.masks]


def entry_barrier(place, far=False):
    barrier = pltpu.get_barrier_semaphore()
    peers = place.everyone(far)
    for peer in peers:
        pl.semaphore_signal(barrier, inc=1, device_id=peer, device_id_type=MESH)
    pl.semaphore_wait(barrier, len(peers))


def column_copies(place, src, dst, sem, block, back=False):
    if block % 128:
        return [pltpu.make_async_copy(src, dst, sem)]
    out = []
    for p in range(place.n_dp):
        natural = pl.ds(pl.multiple_of(place.dp_of(p) * block, block), block)
        here = pl.ds(p * block, block)
        a, b = (here, natural) if back else (natural, here)
        out.append(pltpu.make_async_copy(src.at[:, a], dst.at[:, b], sem))
    return out


def remote(src, dst, send, recv, peer):
    return pltpu.make_async_remote_copy(
        src_ref=src, dst_ref=dst, send_sem=send, recv_sem=recv, device_id=peer, device_id_type=MESH
    )


class Weights:
    def __init__(self, place, sources, full, sems):
        self.place, self.sources, self.full = place, sources, full
        self.z_send, self.z_recv, self.x_send, self.x_recv, self.local = sems
        self.block = sources[0].shape[0]
        self.cols = sources[0].shape[1] // 2
        self.half = place.n_dp // 2

    def rows(self, position, count=1):
        return pl.ds(pl.multiple_of(position * self.block, self.block), count * self.block)

    def source(self, g, half):
        return self.sources[g].at[:, pl.ds(pl.multiple_of(half * self.cols, self.cols), self.cols)]

    def start(self, g):
        place = self.place
        z = place.z
        own = pltpu.make_async_copy(self.source(g, z), self.full.at[g, self.rows(z), :], self.local.at[g])
        own.start()
        remote(
            self.source(g, z),
            self.full.at[g, self.rows(z + self.half), :],
            self.x_send.at[g],
            self.x_recv.at[g],
            place.x_peer(),
        ).start()
        for i, (bits, above, flips) in reversed(list(enumerate(place.masks))):
            half = 1 - z if flips else z
            remote(
                self.source(g, half),
                self.full.at[g, self.rows(z + above), :],
                self.z_send.at[g],
                self.z_recv.at[g, i],
                place.peer(bits),
            ).start()

    def forward(self, g, i):
        place = self.place
        bits, above, flips = place.masks[i]
        position = (1 - place.z if flips else place.z) + above
        here = self.full.at[g, self.rows(position), :]
        remote(here, here, self.z_send.at[g], self.z_recv.at[g, i], place.peer(bits)).wait_recv()
        remote(
            here,
            self.full.at[g, self.rows(position + self.half), :],
            self.x_send.at[g],
            self.x_recv.at[g],
            place.x_peer(),
        ).start()

    def forward_all(self, g):
        for i in range(len(self.place.masks)):
            self.forward(g, i)

    def finish(self, g):
        z = self.place.z
        pltpu.make_async_copy(self.source(g, z), self.full.at[g, self.rows(z), :], self.local.at[g]).wait()
        there = self.full.at[g, self.rows(self.half, self.half), :]
        remote(there, there, self.x_send.at[g], self.x_recv.at[g], self.place.x_peer()).wait_recv()

    def sent(self, g):
        there = self.full.at[g, self.rows(self.half, self.half), :]
        remote(there, there, self.x_send.at[g], self.x_recv.at[g], self.place.x_peer()).wait_send()
        count = self.half - 1
        those = self.full.at[g, self.rows(0, count), :]
        remote(those, those, self.z_send.at[g], self.z_recv.at[g, 0], self.place.x_peer()).wait_send()


class Gather:
    def __init__(self, place, buffer, send, recv):
        self.place, self.buffer = place, buffer
        self.send, self.recv = send, recv
        self.tokens = buffer.shape[0] // 8
        self.peers = {1: place.c_peer(), 2: place.y_peer(), 4: place.z_peer()}

    def slot(self, s):
        return self.buffer.at[pl.ds(pl.multiple_of(s * self.tokens, self.tokens), self.tokens), :]

    def copy(self, source, bit, src=None):
        s = source + bit
        return remote(self.slot(source) if src is None else src, self.slot(s), self.send.at[s - 1], self.recv.at[s - 1], self.peers[bit])

    def start(self, src=None):
        for bit in (4, 2, 1):
            self.copy(0, bit, src).start()

    def from_z(self):
        self.copy(0, 4).wait_recv()
        self.copy(4, 2).start()
        self.copy(4, 1).start()

    def from_y(self):
        self.copy(0, 2).wait_recv()
        self.copy(2, 1).start()

    def from_zy(self):
        self.copy(4, 2).wait_recv()
        self.copy(6, 1).start()

    def chip(self, source):
        self.copy(source, 1).wait_recv()

    def sent(self, src=None):
        self.copy(0, 4, src).wait_send()
        self.copy(0, 2, src).wait_send()
        self.copy(0, 1, src).wait_send()
        self.copy(4, 2).wait_send()
        self.copy(4, 1).wait_send()
        self.copy(2, 1).wait_send()
        self.copy(6, 1).wait_send()


class Scatter:
    def __init__(self, place, keep, c_out, c_in, far_out, far_in, sems):
        self.place = place
        self.keep, self.c_out, self.c_in, self.far_out, self.far_in = keep, c_out, c_in, far_out, far_in
        self.c_send, self.c_recv, self.far_send, self.far_recv = sems
        self.tokens = c_out.shape[1]

    def part(self, b, value):
        self.keep[b] = value[: self.tokens].astype(self.keep.dtype)
        self.c_out[b] = value[self.tokens :].astype(BF)
        self.c_copy(b).start()

    def c_copy(self, b):
        return remote(self.c_out.at[b], self.c_in.at[b], self.c_send.at[b], self.c_recv.at[b], self.place.c_peer())

    def far_copy(self, b):
        peer = self.place.z_peer() if b == 2 else self.place.y_peer()
        return remote(
            self.far_source(b), self.far_in.at[b - 1], self.far_send.at[b - 1], self.far_recv.at[b - 1], peer
        )

    def far_source(self, b):
        return self.keep.at[b] if self.far_out is None else self.far_out.at[b - 1]

    def rows(self, body, step=16):
        def loop(i, carry):
            body(pl.ds(pl.multiple_of(i * step, step), step))
            return carry

        lax.fori_loop(0, self.tokens // step, loop, 0)

    def pass_on(self, b):
        self.c_copy(b).wait_recv()
        if b == 2:
            self.far_copy(3).wait_recv()

        def body(r):
            total = self.keep[b, r, :].astype(F32) + self.c_in[b, r, :].astype(F32)
            if b == 2:
                total = total + self.far_in[2, r, :].astype(F32)
            self.far_source(b)[r, :] = total.astype(BF)

        self.rows(body)
        self.far_copy(b).start()

    def wait_own(self):
        self.c_copy(0).wait_recv()
        self.far_copy(1).wait_recv()
        self.far_copy(2).wait_recv()

    def own(self, r):
        return (
            self.keep[0, r, :].astype(F32)
            + self.c_in[0, r, :].astype(F32)
            + self.far_in[0, r, :].astype(F32)
            + self.far_in[1, r, :].astype(F32)
        )

    def sent(self):
        for b in range(4):
            self.c_copy(b).wait_send()
        for b in (3, 2, 1):
            self.far_copy(b).wait_send()


def normalized(value):
    center = value - jnp.mean(value, axis=-1, keepdims=True)
    spread = jnp.mean(center * center, axis=-1, keepdims=True)
    return center * lax.rsqrt(spread + EPSILON)


def decay_tile(t, cumul_rows, cumul_here, first, rows, length, tokens):
    square = (rows, rows)
    same = lax.broadcasted_iota(jnp.int32, square, 0) == lax.broadcasted_iota(jnp.int32, square, 1)
    cumul_cols = jnp.sum(jnp.where(same, cumul_here, 0.0), axis=1, keepdims=True)
    index = lax.broadcasted_iota(jnp.int32, (rows, length), 0) + first
    other = lax.broadcasted_iota(jnp.int32, (rows, length), 1)
    at = ((index // tokens) ^ t) * tokens + index % tokens
    to = ((other // tokens) ^ t) * tokens + other % tokens
    causal = at >= to
    return jnp.where(causal, jnp.exp(jnp.where(causal, cumul_cols - cumul_rows, 0.0)), 0.0)


def spread_small(place, own, others, params, group, cumul, block):
    pieces = group.shape[1] // block
    steps = cumul.shape[1] // block
    first = place.z == 0

    def of(above, flips, rows):
        j = place.slot(above, flips)
        return own[rows, :] if j is None else others[j, rows, :]

    head = slice(0, 4)
    for p in range(place.n_dp):
        same, flipped = of(p & ~1, 0, head), of(p & ~1, 1, head)
        params[head, p * block : (p + 1) * block] = jnp.where(place.z == p % 2, same, flipped)

    def head_rows(above, flips, at, count):
        one = of(above, flips, slice(at, at + count))
        two = of(above, flips, slice(at + count, at + 2 * count))
        return jnp.where(first, one, two)

    total = head_rows(0, 0, 4, pieces)
    for bits, above, flips in place.pairs:
        total = total + head_rows(above, flips, 4, pieces)
    for k in range(pieces):
        group[0:1, k * block : (k + 1) * block] = total[k : k + 1, :]
    at = 4 + 2 * pieces
    for row, flips in ((0, 0), (1, 1)):
        value = head_rows(0, flips, at, steps)
        for k in range(steps):
            cumul[row : row + 1, k * block : (k + 1) * block] = value[k : k + 1, :]


def forward_kernel(
    n_dp,
    x_hbm,
    cot_hbm,
    small_ref,
    s_qk,
    s_v,
    s_g,
    s_o,
    s_fg,
    s_fu,
    s_fd,
    w_out,
    normed_out,
    qkv_out,
    gate_out,
    mixed_out,
    ffn_in_out,
    hidden_out,
    grads_out,
    cot_out,
    middle_out,
    params_out,
    group_out,
    cumul_out,
    small_in,
    params_ref,
    group_ref,
    cum_row_ref,
    x_ref,
    w,
    normed_all,
    cot_all,
    ffn_in,
    qkv,
    gate_in,
    mixed,
    gated,
    gate_hidden,
    up_hidden,
    hidden,
    grads,
    middle,
    keep,
    c_out,
    c_in,
    far_out,
    far_in,
    z_send,
    z_recv,
    x_send,
    x_recv,
    w_local,
    ag_send,
    ag_recv,
    c_send,
    c_recv,
    far_send,
    far_recv,
    out_sem,
    small_send,
    small_recv,
):
    place = Place(n_dp)
    tokens, width = x_ref.shape
    block = width // n_dp
    rows_all = 8 * tokens
    length = rows_all // 2
    head_k = qkv.shape[1] // 4
    scale = 1.0 / math.sqrt(head_k)
    tile = 2 * tokens
    weights = Weights(place, [s_qk, s_v, s_g, s_o, s_fg, s_fu, s_fd], w, (z_send, z_recv, x_send, x_recv, w_local))
    ag_normed = Gather(place, normed_all, ag_send.at[0], ag_recv.at[0])
    ag_cot = Gather(place, cot_all, ag_send.at[1], ag_recv.at[1])
    ag_two = Gather(place, ffn_in, ag_send.at[2], ag_recv.at[2])
    branch = Scatter(place, keep, c_out, c_in, far_out, far_in, (c_send, c_recv, far_send, far_recv))
    outs = []

    def save(src, dst, index):
        copy = pltpu.make_async_copy(src, dst, out_sem.at[index])
        copy.start()
        outs.append(copy)

    def over(count, step, body):
        def loop(i, carry):
            body(pl.ds(pl.multiple_of(i * step, step), step), i)
            return carry

        lax.fori_loop(0, count // step, loop, 0)

    for copy in column_copies(place, x_hbm, x_ref, out_sem.at[16], block):
        copy.start()
    for copy in column_copies(place, cot_hbm, ag_cot.slot(0), out_sem.at[17], block):
        copy.start()
    entry_barrier(place, True)
    small = []
    for j, (bits, above, flips) in enumerate(place.pairs):
        copy = remote(small_ref, small_in.at[j], small_send.at[j], small_recv.at[j], place.peer(bits))
        copy.start()
        small.append(copy)
    weights.start(QK)
    pltpu.make_async_copy(x_hbm, x_ref, out_sem.at[16]).wait()
    for copy in small:
        copy.wait()
    spread_small(place, small_ref, small_in, params_ref, group_ref, cum_row_ref, block)

    def first_norm(r, i):
        value = normalized(x_ref[r, :].astype(F32))
        normed_all[r, :] = (value * params_ref[0:1, :] + params_ref[2:3, :]).astype(BF)

    over(tokens, 16, first_norm)
    ag_normed.start()
    save(params_ref, params_out, 18)
    save(group_ref, group_out, 19)
    save(cum_row_ref, cumul_out, 20)
    pltpu.make_async_copy(cot_hbm, ag_cot.slot(0), out_sem.at[17]).wait()
    weights.start(V)
    weights.start(G)
    weights.forward_all(QK)
    ag_normed.from_z()
    ag_normed.from_y()
    ag_cot.start()
    weights.start(O)
    ag_normed.from_zy()
    for s in (0, 2, 4, 6):
        ag_normed.chip(s)
    save(normed_all, normed_out, 0)
    weights.finish(QK)

    def make_qk(r, i):
        qkv[r, : 2 * head_k] = dot_nn(normed_all[r, :], w[QK]).astype(BF)

    over(rows_all, tile, make_qk)
    save(w.at[QK], w_out.at[QK], 1)
    weights.start(FG)
    weights.forward_all(V)
    weights.finish(V)

    def make_v(r, i):
        qkv[r, 2 * head_k :] = dot_nn(normed_all[r, :], w[V]).astype(BF)

    over(rows_all, tile, make_v)
    save(w.at[V], w_out.at[V], 2)
    save(qkv, qkv_out, 3)
    weights.start(FU)

    def retention(r, i):
        start = pl.multiple_of((i // 2) * length, length)
        seq = pl.ds(start, length)
        scores = dot_nt(qkv[r, :head_k], qkv[seq, head_k : 2 * head_k])
        here = cum_row_ref[pl.ds(i // 2, 1), pl.ds(pl.multiple_of((i % 2) * tile, tile), tile)]
        decays = decay_tile(
            place.t, cum_row_ref[pl.ds(i // 2, 1), :], here, (i % 2) * tile, tile, length, tokens
        )
        weighted = (scores * decays * scale).astype(BF)
        mixed[r, :] = dot_nn(weighted, qkv[seq, 2 * head_k :])

    over(rows_all, tile, retention)
    save(mixed, mixed_out, 4)
    weights.forward_all(G)
    ag_cot.from_z()
    ag_cot.from_y()
    weights.finish(G)

    def gating(r, i):
        gate = dot_nn(normed_all[r, :], w[G])
        gate_in[r, :] = gate
        value = mixed[r, :]
        center = value - jnp.mean(value, axis=-1, keepdims=True)
        spread = jnp.mean(center * center, axis=-1, keepdims=True)
        flat = center * lax.rsqrt(jnp.maximum(spread, GROUP_FLOOR)) * group_ref[...]
        gated[r, :] = (flat * (gate * lax.logistic(gate))).astype(BF)

    over(rows_all, tile, gating)
    save(w.at[G], w_out.at[G], 5)
    save(gate_in, gate_out, 6)
    weights.forward_all(O)
    ag_cot.from_zy()
    weights.finish(O)

    def branch_part(i, carry):
        r = pl.ds(pl.multiple_of((3 - i) * tile, tile), tile)
        branch.part(3 - i, dot_nt(gated[r, :], w[O]))
        return carry

    lax.fori_loop(0, 4, branch_part, 0)
    save(w.at[O], w_out.at[O], 7)
    branch.pass_on(3)
    branch.pass_on(1)
    for s in (0, 2, 4, 6):
        ag_cot.chip(s)
    save(cot_all, cot_out, 8)
    weights.forward_all(FG)
    branch.pass_on(2)
    weights.start(FD)
    weights.forward(FU, 0)
    branch.wait_own()

    def second_norm(r, i):
        value = x_ref[r, :].astype(F32) + branch.own(r)
        middle[r, :] = value
        ffn_in[r, :] = (normalized(value) * params_ref[1:2, :] + params_ref[3:4, :]).astype(BF)

    over(tokens, 16, second_norm)
    ag_two.start()
    save(middle, middle_out, 9)
    for i in range(1, len(place.masks)):
        weights.forward(FU, i)
    weights.finish(FG)
    weights.finish(FU)

    def feed(b):
        r = pl.ds(pl.multiple_of(b * tile, tile), tile)
        gate = dot_nn(ffn_in[r, :], w[FG])
        up = dot_nn(ffn_in[r, :], w[FU])
        gate_hidden[r, :] = gate
        up_hidden[r, :] = up
        hidden[r, :] = (gelu(gate) * up).astype(BF)

    ag_two.from_z()
    ag_two.from_y()

    def feed_chips(b, carry):
        ag_two.chip(2 * b)
        feed(b)
        return carry

    lax.fori_loop(0, 3, feed_chips, 0)
    weights.forward(FD, len(place.masks) - 1)
    ag_two.from_zy()
    lax.fori_loop(3, 4, feed_chips, 0)
    save(w.at[FG], w_out.at[FG], 10)
    save(w.at[FU], w_out.at[FU], 11)
    save(ffn_in, ffn_in_out, 12)
    save(hidden, hidden_out, 13)
    for i in reversed(range(len(place.masks) - 1)):
        weights.forward(FD, i)
    weights.finish(FD)
    save(w.at[FD], w_out.at[FD], 14)
    size = gate_hidden.shape[1]

    def feed_back(r, i):
        back = dot_nn(cot_all[r, :], w[FD])
        gate = gate_hidden[r, :]
        value, slope = gelu_and_slope(gate)
        grads[r, :size] = (back * up_hidden[r, :] * slope).astype(BF)
        grads[r, size:] = (back * value).astype(BF)

    over(rows_all, tile, feed_back)
    save(grads, grads_out, 15)
    for copy in outs:
        copy.wait()
    for g in range(GROUPS):
        weights.sent(g)
    ag_normed.sent()
    ag_cot.sent()
    ag_two.sent()
    branch.sent()


ROOT = math.sqrt(2.0 / math.pi)


def gelu(v):
    return 0.5 * v * (1.0 + jnp.tanh(ROOT * (v + 0.044715 * v * v * v)))


def gelu_and_slope(v):
    inside = jnp.tanh(ROOT * (v + 0.044715 * v * v * v))
    slope = 0.5 * (1.0 + inside) + 0.5 * v * (1.0 - inside * inside) * ROOT * (1.0 + 3 * 0.044715 * v * v)
    return 0.5 * v * (1.0 + inside), slope


def forward_call(n_dp, x, cot, small, sources):
    tokens, width = x.shape
    length = 4 * tokens
    rows_all = 8 * tokens
    cols = sources[0].shape[1] // 2
    masks = n_dp // 2 - 1
    vmem, hbm = pl.BlockSpec(memory_space=pltpu.VMEM), pl.BlockSpec(memory_space=pl.ANY)
    shape = jax.ShapeDtypeStruct
    outs = (
        shape((GROUPS, width, cols), BF),
        shape((rows_all, width), BF),
        shape((rows_all, 2 * cols), BF),
        shape((rows_all, cols), F32),
        shape((rows_all, cols), F32),
        shape((rows_all, width), BF),
        shape((rows_all, cols), BF),
        shape((rows_all, 2 * cols), BF),
        shape((rows_all, width), BF),
        shape((tokens, width), F32),
        shape((8, width), F32),
        shape((1, cols), F32),
        shape((2, length), F32),
    )
    dma = pltpu.SemaphoreType.DMA
    scratch = [
        pltpu.VMEM((n_dp - 1, *small.shape), F32),
        pltpu.VMEM((8, width), F32),
        pltpu.VMEM((1, cols), F32),
        pltpu.VMEM((2, length), F32),
        pltpu.VMEM((tokens, width), BF),
        pltpu.VMEM((GROUPS, width, cols), BF),
        pltpu.VMEM((rows_all, width), BF),
        pltpu.VMEM((rows_all, width), BF),
        pltpu.VMEM((rows_all, width), BF),
        pltpu.VMEM((rows_all, 2 * cols), BF),
        pltpu.VMEM((rows_all, cols), F32),
        pltpu.VMEM((rows_all, cols), F32),
        pltpu.VMEM((rows_all, cols), BF),
        pltpu.VMEM((rows_all, cols), F32),
        pltpu.VMEM((rows_all, cols), F32),
        pltpu.VMEM((rows_all, cols), BF),
        pltpu.VMEM((rows_all, 2 * cols), BF),
        pltpu.VMEM((tokens, width), F32),
        pltpu.VMEM((4, tokens, width), F32),
        pltpu.VMEM((4, tokens, width), BF),
        pltpu.VMEM((4, tokens, width), BF),
        pltpu.VMEM((3, tokens, width), BF),
        pltpu.VMEM((3, tokens, width), BF),
        dma((GROUPS,)),
        dma((GROUPS, masks)),
        dma((GROUPS,)),
        dma((GROUPS,)),
        dma((GROUPS,)),
        dma((3, 7)),
        dma((3, 7)),
        dma((4,)),
        dma((4,)),
        dma((3,)),
        dma((3,)),
        dma((21,)),
        dma((n_dp - 1,)),
        dma((n_dp - 1,)),
    ]
    return pl.pallas_call(
        functools.partial(forward_kernel, n_dp),
        out_shape=outs,
        in_specs=[hbm, hbm, vmem] + [hbm] * GROUPS,
        out_specs=(hbm,) * len(outs),
        scratch_shapes=scratch,
        compiler_params=pltpu.CompilerParams(
            collective_id=1, has_side_effects=True, vmem_limit_bytes=64_000_000
        ),
    )(x, cot, small, *sources)


class Reduce:
    def __init__(self, place, keep, x_out, x_in, z_in, own_out, sems, own_sem):
        self.place = place
        self.keep, self.x_out, self.x_in, self.z_in, self.own_out = keep, x_out, x_in, z_in, own_out
        self.x_send, self.x_recv, self.z_send, self.z_recv = sems
        self.own_sem = own_sem
        self.block = z_in.shape[2]
        self.half = place.n_dp // 2
        z = place.z
        self.targets = [
            ((1 - z if flips else z) + above, i, place.peer(bits)) for i, (bits, above, flips) in enumerate(place.masks)
        ]
        self.targets.reverse()

    def rows(self, position):
        return pl.ds(pl.multiple_of(position * self.block, self.block), self.block)

    def x_copy(self, g, ring, position):
        return remote(
            self.x_out.at[ring, self.rows(position), :],
            self.x_in.at[g, self.rows(position), :],
            self.x_send.at[g],
            self.x_recv.at[g, position],
            self.place.x_peer(),
        )

    def z_copy(self, g, position, i, peer):
        return remote(
            self.keep.at[g, self.rows(position), :],
            self.z_in.at[g, i],
            self.z_send.at[g],
            self.z_recv.at[g, i],
            peer,
        )

    def upper(self, g, ring, left, right, col, step):
        width = left.shape[1] // 2
        cols = self.keep.shape[2]

        def body(i, carry):
            at = pl.multiple_of(i * step, step)
            value = dot_tn(left[:, pl.ds(pl.multiple_of(width + at, step), step)], right[:, col : col + cols])
            self.x_out[ring, pl.ds(at, step), :] = value.astype(BF)
            return carry

        lax.fori_loop(0, width // step, body, 0)
        for position, _, _ in self.targets:
            self.x_copy(g, ring, position).start()
        self.x_copy(g, ring, self.place.z).start()

    def lower(self, g, left, right, col, step):
        width = left.shape[1] // 2
        cols = self.keep.shape[2]

        def body(i, carry):
            at = pl.ds(pl.multiple_of(i * step, step), step)
            self.keep[g, at, :] = dot_tn(left[:, at], right[:, col : col + cols]).astype(BF)
            return carry

        lax.fori_loop(0, width // step, body, 0)

    def x_sent(self, g, ring):
        whole = self.x_out.at[ring]
        remote(whole, whole, self.x_send.at[g], self.x_recv.at[g, 0], self.place.x_peer()).wait_send()

    def add(self, g, ring, position):
        self.x_copy(g, ring, position).wait_recv()
        step = min(64, self.block)

        def body(i, carry):
            r = pl.ds(pl.multiple_of(position * self.block + i * step, step), step)
            self.keep[g, r, :] = (self.keep[g, r, :].astype(F32) + self.x_in[g, r, :].astype(F32)).astype(BF)
            return carry

        lax.fori_loop(0, self.block // step, body, 0)

    def own_copy(self, g):
        return pltpu.make_async_copy(
            self.keep.at[g, self.rows(self.place.z), :], self.own_out.at[g], self.own_sem.at[g]
        )

    def pass_on(self, g, ring):
        for position, i, peer in self.targets:
            self.add(g, ring, position)
            self.z_copy(g, position, i, peer).start()
        self.add(g, ring, self.place.z)
        self.own_copy(g).start()

    def finish(self, g):
        self.own_copy(g).wait()
        for position, i, peer in self.targets:
            self.z_copy(g, position, i, peer).wait()


def norm_back(value, grad, gain):
    center = value - jnp.mean(value, axis=-1, keepdims=True)
    spread = jnp.mean(center * center, axis=-1, keepdims=True)
    r = lax.rsqrt(spread + EPSILON)
    hat = center * r
    scaled = grad * gain
    back = r * (
        scaled - jnp.mean(scaled, axis=-1, keepdims=True) - hat * jnp.mean(scaled * hat, axis=-1, keepdims=True)
    )
    return back, jnp.sum(grad * hat, axis=0, keepdims=True), jnp.sum(grad, axis=0, keepdims=True)


def backward_kernel(
    n_dp,
    x_hbm,
    params_ref,
    group_ref,
    cum_row_ref,
    w_ref,
    normed_ref,
    qkv_ref,
    gate_ref,
    mixed_ref,
    ffn_in_ref,
    hidden_ref,
    grads_ref,
    cot_ref,
    middle_ref,
    layer_out,
    input_grad_out,
    own_out,
    z_in,
    sums_out,
    w,
    tokens_a,
    ffn_in,
    branch_all,
    slim,
    qkv,
    gate_in,
    mixed,
    gated,
    x_ref,
    middle,
    grad_middle,
    sums,
    sums_in,
    group_sum,
    payload,
    payload_in,
    keep,
    c_out,
    c_in,
    far_in,
    c_in_two,
    far_in_two,
    dw_keep,
    x_out,
    x_in,
    ag_send,
    ag_recv,
    c_send,
    c_recv,
    far_send,
    far_recv,
    x_send,
    x_recv,
    z_send,
    z_recv,
    load_sem,
    own_sem,
    sum_send,
    sum_recv,
    pay_send,
    pay_recv,
):
    place = Place(n_dp)
    tokens, width = x_ref.shape
    rows_all = 8 * tokens
    length = rows_all // 2
    cols = gated.shape[1]
    head_k = cols // 2
    scale = 1.0 / math.sqrt(head_k)
    tile = 2 * tokens
    step = min(512, width // 2)
    block = z_in.shape[2]
    ag = Gather(place, branch_all, ag_send, ag_recv)

    def scatter(k, c, far):
        return Scatter(place, keep, c_out, c, None, far, (c_send.at[k], c_recv.at[k], far_send.at[k], far_recv.at[k]))

    rs_two = scatter(0, c_in, far_in)
    rs_out = scatter(1, c_in_two, far_in_two)
    rs_one = scatter(2, c_in, far_in)
    dw = Reduce(place, dw_keep, x_out, x_in, z_in, own_out, (x_send, x_recv, z_send, z_recv), own_sem)
    result = ffn_in.at[:tokens, :]
    weighted = ffn_in.at[tokens : tokens + length, :length]
    score_back = ffn_in.at[tokens : tokens + length, length : 2 * length]
    ring = {FD: 0, FG: 1, FU: 2, O: 3, QK: 0, V: 1, G: 2}

    def load(src, dst, index):
        copy = pltpu.make_async_copy(src, dst, load_sem.at[index])
        copy.start()
        return copy

    def over(count, size, body):
        def loop(i, carry):
            body(pl.ds(pl.multiple_of(i * size, size), size), i)
            return carry

        lax.fori_loop(0, count // size, loop, 0)

    in_cot = load(cot_ref, tokens_a, 3)
    in_hidden = load(hidden_ref, slim.at[:, 2 * cols :], 4)
    in_grads = load(grads_ref, slim.at[:, : 2 * cols], 0)
    in_fg = load(w_ref.at[FG], w.at[0], 1)
    in_fu = load(w_ref.at[FU], w.at[1], 2)
    in_ffn = load(ffn_in_ref, ffn_in, 5)
    in_middle = load(middle_ref, middle, 6)
    in_mixed = load(mixed_ref, mixed, 7)
    in_gate = load(gate_ref, gate_in, 8)
    in_o = load(w_ref.at[O], w.at[2], 9)
    in_qkv = load(qkv_ref, qkv, 10)
    for copy in column_copies(place, x_hbm, x_ref, load_sem.at[11], block):
        copy.start()
    sums[...] = jnp.zeros_like(sums)
    group_sum[...] = jnp.zeros_like(group_sum)
    entry_barrier(place, True)
    in_cot.wait()
    in_hidden.wait()
    dw.upper(FD, ring[FD], tokens_a, slim, 2 * cols, step)
    in_grads.wait()
    in_fg.wait()
    in_fu.wait()

    def rows_of(i):
        return 3 - i, pl.ds(pl.multiple_of((3 - i) * tile, tile), tile)

    def two_part(i, carry):
        b, r = rows_of(i)
        rs_two.part(b, dot_nt(slim[r, :cols], w[0]) + dot_nt(slim[r, cols : 2 * cols], w[1]))
        return carry

    lax.fori_loop(0, 4, two_part, 0)
    in_fd = load(w_ref.at[FD], w.at[0], 1)
    in_qk = load(w_ref.at[QK], w.at[1], 2)
    rs_two.pass_on(3)
    rs_two.pass_on(1)
    in_ffn.wait()
    dw.upper(FG, ring[FG], ffn_in, slim, 0, step)
    dw.upper(FU, ring[FU], ffn_in, slim, cols, step)
    dw.lower(FD, tokens_a, slim, 2 * cols, step)
    dw.lower(FG, ffn_in, slim, 0, step)
    rs_two.pass_on(2)
    dw.lower(FU, ffn_in, slim, cols, step)
    in_mixed.wait()
    in_gate.wait()

    def gating(r, i):
        value = mixed[r, :]
        center = value - jnp.mean(value, axis=-1, keepdims=True)
        spread = jnp.mean(center * center, axis=-1, keepdims=True)
        gate = gate_in[r, :]
        flat = center * lax.rsqrt(jnp.maximum(spread, GROUP_FLOOR)) * group_ref[...]
        gated[r, :] = (flat * (gate * lax.logistic(gate))).astype(BF)

    over(rows_all, tokens, gating)
    in_middle.wait()
    rs_two.wait_own()

    def second_back(r, i):
        back, gain_sum, bias_sum = norm_back(middle[r, :], rs_two.own(r), params_ref[1:2, :])
        total = tokens_a[r, :].astype(F32) + back
        grad_middle[r, :] = total
        branch_all[r, :] = total.astype(BF)
        sums[1:2, :] += gain_sum
        sums[3:4, :] += bias_sum

    over(tokens, 16, second_back)
    ag.start()
    in_normed = load(normed_ref, tokens_a, 3)
    rs_two.sent()
    in_fd.wait()
    dw.pass_on(FD, ring[FD])

    def out_part(i, carry):
        b, r = rows_of(i)
        rs_out.part(b, dot_nt(slim[r, 2 * cols :], w[0]))
        return carry

    lax.fori_loop(0, 4, out_part, 0)
    in_v = load(w_ref.at[V], w.at[0], 1)
    ag.from_z()
    ag.from_y()
    rs_out.pass_on(3)
    rs_out.pass_on(1)
    in_o.wait()
    in_qkv.wait()

    def gating_back(b):
        r = pl.ds(pl.multiple_of(b * tile, tile), tile)
        back = dot_nn(branch_all[r, :], w[2])
        value = mixed[r, :]
        center = value - jnp.mean(value, axis=-1, keepdims=True)
        spread = jnp.mean(center * center, axis=-1, keepdims=True)
        inverse = lax.rsqrt(jnp.maximum(spread, GROUP_FLOOR))
        hat = center * inverse
        gate = gate_in[r, :]
        sigmoid = lax.logistic(gate)
        flat = hat * group_ref[...]
        slope = sigmoid * (1.0 + gate * (1.0 - sigmoid))
        slim[r, 2 * cols :] = (back * flat * slope).astype(BF)
        grad = back * (gate * sigmoid)
        group_sum[...] += jnp.sum(grad * hat, axis=0, keepdims=True)
        scaled = grad * group_ref[...]
        live = jnp.where(spread > GROUP_FLOOR, 1.0, jnp.where(spread == GROUP_FLOOR, 0.5, 0.0))
        moment = jnp.mean(scaled * hat, axis=-1, keepdims=True) * live
        mixed_back = inverse * (scaled - jnp.mean(scaled, axis=-1, keepdims=True) - hat * moment)
        slim[r, cols : 2 * cols] = mixed_back.astype(BF)

    def sequence_back(s):
        seq = pl.ds(pl.multiple_of(s * length, length), length)

        def body(i, carry):
            r = pl.ds(pl.multiple_of(s * length + i * tile, tile), tile)
            at = pl.ds(pl.multiple_of(i * tile, tile), tile)
            scores = dot_nt(qkv[r, :head_k], qkv[seq, head_k : 2 * head_k])
            here = cum_row_ref[pl.ds(s, 1), at]
            decays = decay_tile(
                place.t, cum_row_ref[pl.ds(s, 1), :], here, i * tile, tile, length, tokens
            )
            weighted[at, :] = (scores * decays * scale).astype(BF)
            back = dot_nt(slim[r, cols : 2 * cols], qkv[seq, 2 * head_k :])
            grad = (back * decays * scale).astype(BF)
            score_back[at, :] = grad
            slim[r, :head_k] = dot_nn(grad, qkv[seq, head_k : 2 * head_k]).astype(BF)
            return carry

        lax.fori_loop(0, length // tile, body, 0)
        slim[seq, head_k : 2 * head_k] = dot_tn(score_back[...], qkv[seq, :head_k]).astype(BF)
        slim[seq, cols : 2 * cols] = dot_tn(weighted[...], slim[seq, cols : 2 * cols]).astype(BF)


    def gating_chips(b, carry):
        ag.chip(2 * b)
        gating_back(b)
        return carry

    lax.fori_loop(0, 2, gating_chips, 0)
    dw.pass_on(FG, ring[FG])
    ag.from_zy()
    lax.fori_loop(2, 4, gating_chips, 0)
    in_g = load(w_ref.at[G], w.at[2], 9)
    dw.upper(O, ring[O], branch_all, gated, 0, step)

    def sequences(s, carry):
        sequence_back(s)
        return carry

    lax.fori_loop(0, 2, sequences, 0)
    in_normed.wait()
    dw.x_sent(FD, ring[FD])
    dw.upper(QK, ring[QK], tokens_a, slim, 0, step)
    dw.x_sent(FG, ring[FG])
    dw.upper(V, ring[V], tokens_a, slim, cols, step)
    dw.lower(O, branch_all, gated, 0, step)
    rs_out.pass_on(2)
    dw.pass_on(FU, ring[FU])
    dw.x_sent(FU, ring[FU])
    dw.upper(G, ring[G], tokens_a, slim, 2 * cols, step)
    dw.lower(QK, tokens_a, slim, 0, step)
    dw.lower(V, tokens_a, slim, cols, step)
    dw.lower(G, tokens_a, slim, 2 * cols, step)
    rs_out.wait_own()

    def finish_out(r, i):
        result[r, :] = (middle[r, :] + rs_out.own(r)).astype(BF)

    over(tokens, 16, finish_out)
    out_layer = load(result, layer_out, 4)
    rs_out.sent()
    in_qk.wait()
    in_v.wait()
    in_g.wait()

    def one_part(i, carry):
        b, r = rows_of(i)
        total = dot_nt(slim[r, :cols], w[1]) + dot_nt(slim[r, cols : 2 * cols], w[0])
        rs_one.part(b, total + dot_nt(slim[r, 2 * cols :], w[2]))
        return carry

    lax.fori_loop(0, 4, one_part, 0)
    rs_one.pass_on(3)
    rs_one.pass_on(1)
    dw.pass_on(O, ring[O])
    rs_one.pass_on(2)
    dw.pass_on(QK, ring[QK])
    out_layer.wait()
    rs_one.wait_own()

    pltpu.make_async_copy(x_hbm, x_ref, load_sem.at[11]).wait()

    def first_back(r, i):
        back, gain_sum, bias_sum = norm_back(x_ref[r, :].astype(F32), rs_one.own(r), params_ref[0:1, :])
        result[r, :] = (grad_middle[r, :] + back).astype(BF)
        sums[0:1, :] += gain_sum
        sums[2:3, :] += bias_sum

    over(tokens, 16, first_back)
    out_grad = load(result, input_grad_out, 4)

    def sum_copy(k, peer):
        return remote(sums, sums_in.at[k], sum_send.at[k], sum_recv.at[k], peer)

    for k, peer in enumerate((place.c_peer(), place.y_peer())):
        sum_copy(k, peer).start()
        sum_copy(k, peer).wait()
        sums[...] += sums_in[k]
    pieces = cols // block
    for p in range(n_dp):
        payload[p, 0:4, :] = sums[0:4, p * block : (p + 1) * block]
        for k in range(pieces):
            payload[p, 4 + k : 5 + k, :] = group_sum[0:1, k * block : (k + 1) * block]
    pay = []
    for j, (bits, above, flips) in enumerate(place.pairs):
        position = (1 - place.z if flips else place.z) + above
        copy = remote(payload.at[position], payload_in.at[j], pay_send.at[j], pay_recv.at[j], place.peer(bits))
        copy.start()
        pay.append(copy)
    dw.pass_on(V, ring[V])
    for copy in pay:
        copy.wait()
    mine = payload[place.z]
    other = jnp.zeros_like(mine)
    for j, (bits, above, flips) in enumerate(place.pairs):
        if flips:
            other = other + payload_in[j]
        else:
            mine = mine + payload_in[j]
    sums_out[0] = mine
    sums_out[1] = other
    dw.pass_on(G, ring[G])
    out_grad.wait()
    for g in (O, QK, V, G):
        dw.x_sent(g, ring[g])
    ag.sent()
    rs_one.sent()
    for g in (FD, FG, FU, O, QK, V, G):
        dw.finish(g)


def backward_call(n_dp, x, params, group, cum_row, saved):
    tokens, width = x.shape
    rows_all = 8 * tokens
    w = saved[0]
    cols = w.shape[2]
    block = width // n_dp
    masks = n_dp // 2 - 1
    vmem, hbm = pl.BlockSpec(memory_space=pltpu.VMEM), pl.BlockSpec(memory_space=pl.ANY)
    shape = jax.ShapeDtypeStruct
    pay_rows = -(-(4 + cols // block) // 8) * 8
    outs = (
        shape((tokens, width), BF),
        shape((tokens, width), BF),
        shape((GROUPS, block, cols), BF),
        shape((GROUPS, masks, block, cols), BF),
        shape((2, pay_rows, block), F32),
    )
    dma = pltpu.SemaphoreType.DMA
    scratch = [
        pltpu.VMEM((3, width, cols), BF),
        pltpu.VMEM((rows_all, width), BF),
        pltpu.VMEM((rows_all, width), BF),
        pltpu.VMEM((rows_all, width), BF),
        pltpu.VMEM((rows_all, 3 * cols), BF),
        pltpu.VMEM((rows_all, 2 * cols), BF),
        pltpu.VMEM((rows_all, cols), F32),
        pltpu.VMEM((rows_all, cols), F32),
        pltpu.VMEM((rows_all, cols), BF),
        pltpu.VMEM((tokens, width), BF),
        pltpu.VMEM((tokens, width), F32),
        pltpu.VMEM((tokens, width), F32),
        pltpu.VMEM((8, width), F32),
        pltpu.VMEM((2, 8, width), F32),
        pltpu.VMEM((1, cols), F32),
        pltpu.VMEM((n_dp, pay_rows, block), F32),
        pltpu.VMEM((n_dp - 1, pay_rows, block), F32),
        pltpu.VMEM((4, tokens, width), BF),
        pltpu.VMEM((4, tokens, width), BF),
        pltpu.VMEM((4, tokens, width), BF),
        pltpu.VMEM((3, tokens, width), BF),
        pltpu.VMEM((4, tokens, width), BF),
        pltpu.VMEM((3, tokens, width), BF),
        pltpu.VMEM((GROUPS, width // 2, cols), BF),
        pltpu.VMEM((4, width // 2, cols), BF),
        pltpu.VMEM((GROUPS, width // 2, cols), BF),
        dma((7,)),
        dma((7,)),
        dma((3, 4)),
        dma((3, 4)),
        dma((3, 3)),
        dma((3, 3)),
        dma((GROUPS,)),
        dma((GROUPS, n_dp // 2)),
        dma((GROUPS,)),
        dma((GROUPS, masks)),
        dma((12,)),
        dma((GROUPS,)),
        dma((2,)),
        dma((2,)),
        dma((n_dp - 1,)),
        dma((n_dp - 1,)),
    ]
    return pl.pallas_call(
        functools.partial(backward_kernel, n_dp),
        out_shape=outs,
        in_specs=[hbm, vmem, vmem, vmem] + [hbm] * len(saved),
        out_specs=(hbm,) * 4 + (vmem,),
        scratch_shapes=scratch,
        compiler_params=pltpu.CompilerParams(
            collective_id=2, has_side_effects=True, vmem_limit_bytes=67_000_000
        ),
    )(x, params, group, cum_row, *saved)


def finish_kernel(
    n_dp,
    own_ref,
    others_ref,
    layer_ref,
    grad_ref,
    sums_ref,
    layer_out,
    input_grad,
    query_grad,
    key_grad,
    value_grad,
    gate_grad,
    out_grad,
    group_grad,
    gain_grad,
    bias_grad,
    ffn_gate_grad,
    ffn_up_grad,
    ffn_down_grad,
    own,
    others,
    rows,
    wide,
    tall,
    in_sem,
    out_sem,
    row_sem,
):
    place = Place(n_dp)
    z = place.z
    block, cols = own.shape[1:]
    loads = []
    for g in (FD, FG, FU, O, QK, V, G):
        pair = (
            pltpu.make_async_copy(own_ref.at[g], own.at[g], in_sem.at[0, g]),
            pltpu.make_async_copy(others_ref.at[g], others.at[g], in_sem.at[1, g]),
        )
        for copy in pair:
            copy.start()
        loads.append((g, pair))
    row_loads = [
        pltpu.make_async_copy(layer_ref, rows.at[0], row_sem.at[0]),
        pltpu.make_async_copy(grad_ref, rows.at[1], row_sem.at[1]),
    ]
    for copy in row_loads:
        copy.start()
    outs = []

    def save(src, dst, index):
        copy = pltpu.make_async_copy(src, dst, out_sem.at[index])
        copy.start()
        outs.append(copy)

    wide_at = {FG: 0, FU: 1, V: 2, G: 3, QK: 4}
    tall_at = {FD: 0, O: 1}
    targets = {FG: ffn_gate_grad, FU: ffn_up_grad, V: value_grad, G: gate_grad, FD: ffn_down_grad, O: out_grad}
    for g, pair in loads:
        for copy in pair:
            copy.wait()
        mine = own[g].astype(F32)
        theirs = None
        for i, (bits, above, flips) in enumerate(place.masks):
            value = others[g, i].astype(F32)
            if not flips:
                mine = mine + value
            else:
                theirs = value if theirs is None else theirs + value
        if g in tall_at:
            k = tall_at[g]
            tall[k, pl.ds(pl.multiple_of(z * cols, cols), cols), :] = mine.T
            tall[k, pl.ds(pl.multiple_of((1 - z) * cols, cols), cols), :] = theirs.T
            save(tall.at[k], targets[g], k)
            continue
        k = wide_at[g]
        if g == QK:
            half = cols // 2
            for which, dst in ((0, query_grad), (1, key_grad)):
                part = slice(which * half, (which + 1) * half)
                at = which * cols
                wide[k, :, pl.ds(pl.multiple_of(at + z * half, half), half)] = mine[:, part]
                wide[k, :, pl.ds(pl.multiple_of(at + (1 - z) * half, half), half)] = theirs[:, part]
                save(wide.at[k, :, pl.ds(at, cols)], dst, 2 + which)
            continue
        wide[k, :, pl.ds(pl.multiple_of(z * cols, cols), cols)] = mine
        wide[k, :, pl.ds(pl.multiple_of((1 - z) * cols, cols), cols)] = theirs
        save(wide.at[k], targets[g], 4 + k)
    for k, dst in ((0, layer_out), (1, input_grad)):
        row_loads[k].wait()
        for copy in column_copies(place, rows.at[k], dst, row_sem.at[k], block, True):
            copy.start()
    norm = sums_ref[0, 0:4, :] + sums_ref[1, 0:4, :]
    piece = gain_grad.shape[1]
    mine = norm[:, :piece]
    for k in range(1, block // piece):
        mine = jnp.where(place.t == k, norm[:, k * piece : (k + 1) * piece], mine)
    gain_grad[...] = mine[0:2, :]
    bias_grad[...] = mine[2:4, :]
    piece = group_grad.shape[1]
    here = place.d % (block // piece)
    row = place.d // (block // piece)

    def group_of(which):
        value = sums_ref[which, 4:5, :]
        for k in range(1, cols // block):
            value = jnp.where(row == k, sums_ref[which, 4 + k : 5 + k, :], value)
        out = value[:, :piece]
        for k in range(1, block // piece):
            out = jnp.where(here == k, value[:, k * piece : (k + 1) * piece], out)
        return out

    same, other = group_of(0), group_of(1)
    group_grad[0:1, :] = jnp.where(z == 0, same, other)
    group_grad[1:2, :] = jnp.where(z == 0, other, same)
    for copy in outs:
        copy.wait()
    for k, dst in ((0, layer_out), (1, input_grad)):
        pltpu.make_async_copy(rows.at[k], dst, row_sem.at[k]).wait()


def finish_call(n_dp, n_tensor, own, others, layer, grad, sums):
    tokens, width = layer.shape
    block, cols = own.shape[1:]
    masks = others.shape[1]
    vmem, hbm = pl.BlockSpec(memory_space=pltpu.VMEM), pl.BlockSpec(memory_space=pl.ANY)
    shape = jax.ShapeDtypeStruct
    rows, wide, tall = shape((tokens, width), BF), shape((block, 2 * cols), F32), shape((2 * cols, block), F32)
    thin, norm = shape((block, cols), F32), shape((2, width // (n_dp * n_tensor)), F32)
    outs = (rows, rows, thin, thin, wide, wide, tall, shape((2, cols // n_dp), F32), norm, norm, wide, wide, tall)
    specs = [vmem if o.shape[0] == 2 else hbm for o in outs]
    dma = pltpu.SemaphoreType.DMA
    return pl.pallas_call(
        functools.partial(finish_kernel, n_dp),
        out_shape=outs,
        in_specs=[hbm, hbm, hbm, hbm, vmem],
        out_specs=tuple(specs),
        scratch_shapes=[
            pltpu.VMEM((GROUPS, block, cols), BF),
            pltpu.VMEM((GROUPS, masks, block, cols), BF),
            pltpu.VMEM((2, tokens, width), BF),
            pltpu.VMEM((5, block, 2 * cols), F32),
            pltpu.VMEM((2, 2 * cols, block), F32),
            dma((2, GROUPS)),
            dma((8,)),
            dma((2,)),
        ],
        compiler_params=pltpu.CompilerParams(vmem_limit_bytes=67_000_000),
    )(own, others, layer, grad, sums)


def per_device(
    n_dp,
    n_tensor,
    inputs,
    cotangent,
    log_decay,
    query_weight,
    key_weight,
    value_weight,
    gate_weight,
    out_weight,
    group_gain,
    norm_gains,
    norm_biases,
    ffn_gate_weight,
    ffn_up_weight,
    ffn_down_weight,
):
    place = Place(n_dp)
    d, t = place.d, place.t
    tokens, width = inputs.shape
    block = width // n_dp
    head_v = value_weight.shape[1] // 2

    def position_of(q):
        out = (q // PAIR) & 1
        for k, bit in enumerate(place.rest):
            out = out + ((d // bit) % 2 ^ ((q // bit) & 1)) * (2 << k)
        return out

    def moved(value, index):
        if block % 128 == 0:
            return value
        return jnp.concatenate(
            [lax.dynamic_slice_in_dim(value, index(p) * block, block, 1) for p in range(n_dp)], axis=1
        )

    def half(value, which, axis):
        size = value.shape[axis] // 2
        return lax.dynamic_slice_in_dim(value, which * size, size, axis)

    cumul = jnp.cumsum(log_decay, axis=1).reshape(2, n_tensor, tokens)
    for bit in (1, 2):
        swapped = jnp.concatenate([cumul[:, j ^ bit : (j ^ bit) + 1] for j in range(n_tensor)], axis=1)
        cumul = jnp.where((t // bit) % 2 == 1, swapped, cumul)
    spread = jnp.tile(group_gain.astype(F32), (1, n_dp))
    spread = jnp.where(lax.broadcasted_iota(jnp.int32, spread.shape, 1) // (head_v // n_dp) == d, spread, 0.0)
    parts = [norm_gains.astype(F32), norm_biases.astype(F32), spread, cumul]
    small = jnp.concatenate([part.reshape(-1, block) for part in parts], axis=0)
    small = jnp.pad(small, ((0, -small.shape[0] % 8), (0, 0)))

    def interleaved(first, second):
        parts = [half(first, 0, 1), half(second, 0, 1), half(first, 1, 1), half(second, 1, 1)]
        return jnp.concatenate(parts, axis=1)

    sources = [
        interleaved(query_weight, key_weight),
        value_weight,
        gate_weight,
        out_weight.T,
        ffn_gate_weight,
        ffn_up_weight,
        ffn_down_weight.T,
    ]

    x, cot = moved(inputs, place.dp_of), moved(cotangent, place.dp_of)
    *saved, params, group, cumul = forward_call(n_dp, x, cot, small, sources)
    layer, grad, own, others, sums = backward_call(n_dp, x, params, group, cumul, saved)
    outs = finish_call(n_dp, n_tensor, own, others, layer, grad, sums)
    return (moved(outs[0], position_of), moved(outs[1], position_of), *outs[2:])


def solution(mesh):
    tokens = P(("dp", "tensor"), None)
    rows, cols, norms = P("dp", "tensor"), P("tensor", "dp"), P(None, "dp")
    sums = P(None, ("dp", "tensor"))
    in_specs = (tokens, tokens, cols, rows, rows, rows, rows, cols, cols, norms, norms, rows, rows, cols)
    out_specs = (tokens, tokens, rows, rows, rows, rows, cols, cols, sums, sums, rows, rows, cols)
    body = functools.partial(per_device, mesh.shape["dp"], mesh.shape["tensor"])
    return jax.shard_map(body, mesh=mesh, in_specs=in_specs, out_specs=out_specs, check_vma=False)
```

profile of v0, /device:TPU:0, one launch (start us, length us, event | category | flops | bytes accessed | tf_op | source)
XLA Modules:
  0.0 459.6 jit_solution(6576794801056102349)
XLA Ops:
  0.7 0.7 convert_element_type.11
  1.4 0.7 convert_element_type.12
  2.1 0.7 reshape.71
  2.8 0.6 reduce-window.6
  3.4 0.2 slice_reduce_fusion
  3.5 0.2 reduce-window.9
  3.7 0.1 broadcast_add_fusion
  3.8 0.1 maximum_select_fusion
  3.9 0.1 maximum_select_fusion.1
  4.0 0.7 tile.4
  4.7 0.1 tile.10
  4.8 0.6 select_maximum_fusion.small_ref
  5.4 2.0 copy.29
  7.4 2.0 copy.30
  9.5 1.1 fusion.1
  10.6 0.9 pad_maximum_fusion.s_qk
  11.5 219.7 %shard_map.237 = (bf16[7,2048,512]{2,1,0:T(8,128)(2,1)}, bf16[1024,2048]{1,0:T(8,128)(2,1)}, bf16[1024,1024]{1,0:T(8,128)(2,1)}, f32[1024,512]{1,0:T(8,128)}, f3...) custom-call(bf16[128,2048]{1,0:T(8,128)(2,1)} %x_hbm.3, ...), custom_call_target="tpu_custom_call" | custom-call | tf_op jit(solution)/shard_map/pallas_call | solution.py:675
  231.2 220.2 %shard_map.238 = (bf16[128,2048]{1,0:T(8,128)(2,1)}, bf16[128,2048]{1,0:T(8,128)(2,1)}, bf16[7,256,512]{2,1,0:T(8,128)(2,1)}, bf16[7,3,256,512]{3,2,1,0:T(8,128)(2,1)}, f32[2,8,256]{2,1,0:T(8,128)}) custom-call(bf16[128,2048]{1,0:T(8,128)(2,1)} %x_hbm.3, f32[8,2048]{1,0:T(8,128)} %get-tuple-element.31.params_ref, f32[1,512]{1,0:T(1,128)} %get-tuple-element.32.group_ref, ...), custom_call_target="tpu_custom_call" | custom-call | tf_op jit(solution)/shard_map/pallas_call | solution.py:1194
  451.4 8.0 %shard_map.239 = (bf16[128,2048]{1,0:T(8,128)(2,1)}, bf16[128,2048]{1,0:T(8,128)(2,1)}, f32[256,512]{1,0:T(8,128)}, f32[256,512]{1,0:T(8,128)}, f32[256,1024]{1,...) custom-call(bf16[7,256,512]{2,1,0:T(8,128)(2,1)} %get-tuple-element., ...), custom_call_target="tpu_custom_call" | custom-call | tf_op jit(solution)/shard_map/pallas_call | solution.py:1337
  (8 shorter events, 0.1 us)
where the time goes:
time: 460 us
  Pallas kernels  448 us (97%)
  local copies, waits for them, and re-layouts  6.86 us (1%)
    pallas_call x1, Pallas kernels, backward_call(): pl.pallas_call(functools.partial(backward_kernel, n_dp), out_shape=outs,...  220 us
    pallas_call x1, Pallas kernels, forward_call(): pl.pallas_call(functools.partial(forward_kernel, n_dp), out_shape=outs, i...  220 us

commit v1 on v0

--- a/solution.py
+++ b/solution.py
@@ -16,6 +16,22 @@
 MESH = pl.DeviceIdType.MESH
 QK, V, G, O, FG, FU, FD = range(7)
 GROUPS = 7
+
+
+FORWARD = (
+    "x2", "x3", "x0", "s01", "s22", "s02", "s21", "s41", "s12", "x1", "f01", "s31", "small", "ln", "f22", "ns",
+    "s03", "f41", "f02", "nfy", "s23", "f12", "x6", "s32", "s13", "f31", "s11", "nfz", "f21", "f03", "f32", "ks",
+    "s33", "s53", "nfzy", "f11", "s43", "s51", "f23", "qk", "f13", "kfz", "f33", "v", "g", "f53", "kfy", "s52",
+    "o", "p3", "f51", "p1", "s61", "x5", "f52", "s42", "p2", "f42", "s63", "kfzy", "x4", "f43", "ln2", "f61", "ts",
+    "feedA", "tfy", "s62", "tfz", "feedB", "f63", "f62", "tfzy", "feedC", "feedD", "back",
+)
+BACKWARD = (
+    "u6", "two", "a3", "l6", "s63", "a1", "a2", "l4", "u4", "lnb", "bs", "u5", "s60", "gat", "l5", "s43", "out",
+    "bfz", "s53", "s61", "bfy", "gbA", "s40", "bfzy", "s52", "s41", "gbB", "u3", "seq0", "seq1", "o3", "u2", "l0",
+    "s42", "s51", "s62", "l2", "u0", "s50", "o1", "l3", "o2", "s32", "u1", "s21", "s23", "s33", "s31", "outf",
+    "one", "s30", "l1", "b3", "b1", "s22", "b2", "s02", "s13", "s01", "lna", "s00", "s10", "s11", "s03", "s20",
+    "sc", "sy", "pay", "s12", "payw",
+)
 
 
 def dot_nn(a, b):
@@ -124,45 +140,46 @@
     def source(self, g, half):
         return self.sources[g].at[:, pl.ds(pl.multiple_of(half * self.cols, self.cols), self.cols)]
 
-    def start(self, g):
-        place = self.place
-        z = place.z
-        own = pltpu.make_async_copy(self.source(g, z), self.full.at[g, self.rows(z), :], self.local.at[g])
-        own.start()
+    def own(self, g):
+        z = self.place.z
+        pltpu.make_async_copy(self.source(g, z), self.full.at[g, self.rows(z), :], self.local.at[g]).start()
         remote(
             self.source(g, z),
             self.full.at[g, self.rows(z + self.half), :],
             self.x_send.at[g],
             self.x_recv.at[g],
-            place.x_peer(),
+            self.place.x_peer(),
         ).start()
-        for i, (bits, above, flips) in reversed(list(enumerate(place.masks))):
-            half = 1 - z if flips else z
+
+    def some(self, third):
+        count = len(self.place.masks)
+        return reversed(range(third * count // 3, (third + 1) * count // 3))
+
+    def start(self, g, third):
+        z = self.place.z
+        for i in self.some(third):
+            bits, above, flips = self.place.masks[i]
             remote(
-                self.source(g, half),
+                self.source(g, 1 - z if flips else z),
                 self.full.at[g, self.rows(z + above), :],
                 self.z_send.at[g],
                 self.z_recv.at[g, i],
-                place.peer(bits),
+                self.place.peer(bits),
             ).start()
 
-    def forward(self, g, i):
-        place = self.place
-        bits, above, flips = place.masks[i]
-        position = (1 - place.z if flips else place.z) + above
-        here = self.full.at[g, self.rows(position), :]
-        remote(here, here, self.z_send.at[g], self.z_recv.at[g, i], place.peer(bits)).wait_recv()
-        remote(
-            here,
-            self.full.at[g, self.rows(position + self.half), :],
-            self.x_send.at[g],
-            self.x_recv.at[g],
-            place.x_peer(),
-        ).start()
-
-    def forward_all(self, g):
-        for i in range(len(self.place.masks)):
-            self.forward(g, i)
+    def forward(self, g, third):
+        for i in self.some(third):
+            bits, above, flips = self.place.masks[i]
+            position = (1 - self.place.z if flips else self.place.z) + above
+            here = self.full.at[g, self.rows(position), :]
+            remote(here, here, self.z_send.at[g], self.z_recv.at[g, i], self.place.peer(bits)).wait_recv()
+            remote(
+                here,
+                self.full.at[g, self.rows(position + self.half), :],
+                self.x_send.at[g],
+                self.x_recv.at[g],
+                self.place.x_peer(),
+            ).start()
 
     def finish(self, g):
         z = self.place.z
@@ -436,51 +453,17 @@
         copy = remote(small_ref, small_in.at[j], small_send.at[j], small_recv.at[j], place.peer(bits))
         copy.start()
         small.append(copy)
-    weights.start(QK)
-    pltpu.make_async_copy(x_hbm, x_ref, out_sem.at[16]).wait()
-    for copy in small:
-        copy.wait()
-    spread_small(place, small_ref, small_in, params_ref, group_ref, cum_row_ref, block)
+    size = gate_hidden.shape[1]
 
     def first_norm(r, i):
         value = normalized(x_ref[r, :].astype(F32))
         normed_all[r, :] = (value * params_ref[0:1, :] + params_ref[2:3, :]).astype(BF)
 
-    over(tokens, 16, first_norm)
-    ag_normed.start()
-    save(params_ref, params_out, 18)
-    save(group_ref, group_out, 19)
-    save(cum_row_ref, cumul_out, 20)
-    pltpu.make_async_copy(cot_hbm, ag_cot.slot(0), out_sem.at[17]).wait()
-    weights.start(V)
-    weights.start(G)
-    weights.forward_all(QK)
-    ag_normed.from_z()
-    ag_normed.from_y()
-    ag_cot.start()
-    weights.start(O)
-    ag_normed.from_zy()
-    for s in (0, 2, 4, 6):
-        ag_normed.chip(s)
-    save(normed_all, normed_out, 0)
-    weights.finish(QK)
-
     def make_qk(r, i):
         qkv[r, : 2 * head_k] = dot_nn(normed_all[r, :], w[QK]).astype(BF)
 
-    over(rows_all, tile, make_qk)
-    save(w.at[QK], w_out.at[QK], 1)
-    weights.start(FG)
-    weights.forward_all(V)
-    weights.finish(V)
-
     def make_v(r, i):
         qkv[r, 2 * head_k :] = dot_nn(normed_all[r, :], w[V]).astype(BF)
-
-    over(rows_all, tile, make_v)
-    save(w.at[V], w_out.at[V], 2)
-    save(qkv, qkv_out, 3)
-    weights.start(FU)
 
     def retention(r, i):
         start = pl.multiple_of((i // 2) * length, length)
@@ -493,13 +476,6 @@
         weighted = (scores * decays * scale).astype(BF)
         mixed[r, :] = dot_nn(weighted, qkv[seq, 2 * head_k :])
 
-    over(rows_all, tile, retention)
-    save(mixed, mixed_out, 4)
-    weights.forward_all(G)
-    ag_cot.from_z()
-    ag_cot.from_y()
-    weights.finish(G)
-
     def gating(r, i):
         gate = dot_nn(normed_all[r, :], w[G])
         gate_in[r, :] = gate
@@ -509,43 +485,15 @@
         flat = center * lax.rsqrt(jnp.maximum(spread, GROUP_FLOOR)) * group_ref[...]
         gated[r, :] = (flat * (gate * lax.logistic(gate))).astype(BF)
 
-    over(rows_all, tile, gating)
-    save(w.at[G], w_out.at[G], 5)
-    save(gate_in, gate_out, 6)
-    weights.forward_all(O)
-    ag_cot.from_zy()
-    weights.finish(O)
-
     def branch_part(i, carry):
         r = pl.ds(pl.multiple_of((3 - i) * tile, tile), tile)
         branch.part(3 - i, dot_nt(gated[r, :], w[O]))
         return carry
 
-    lax.fori_loop(0, 4, branch_part, 0)
-    save(w.at[O], w_out.at[O], 7)
-    branch.pass_on(3)
-    branch.pass_on(1)
-    for s in (0, 2, 4, 6):
-        ag_cot.chip(s)
-    save(cot_all, cot_out, 8)
-    weights.forward_all(FG)
-    branch.pass_on(2)
-    weights.start(FD)
-    weights.forward(FU, 0)
-    branch.wait_own()
-
     def second_norm(r, i):
         value = x_ref[r, :].astype(F32) + branch.own(r)
         middle[r, :] = value
         ffn_in[r, :] = (normalized(value) * params_ref[1:2, :] + params_ref[3:4, :]).astype(BF)
-
-    over(tokens, 16, second_norm)
-    ag_two.start()
-    save(middle, middle_out, 9)
-    for i in range(1, len(place.masks)):
-        weights.forward(FU, i)
-    weights.finish(FG)
-    weights.finish(FU)
 
     def feed(b):
         r = pl.ds(pl.multiple_of(b * tile, tile), tile)
@@ -555,28 +503,6 @@
         up_hidden[r, :] = up
         hidden[r, :] = (gelu(gate) * up).astype(BF)
 
-    ag_two.from_z()
-    ag_two.from_y()
-
-    def feed_chips(b, carry):
-        ag_two.chip(2 * b)
-        feed(b)
-        return carry
-
-    lax.fori_loop(0, 3, feed_chips, 0)
-    weights.forward(FD, len(place.masks) - 1)
-    ag_two.from_zy()
-    lax.fori_loop(3, 4, feed_chips, 0)
-    save(w.at[FG], w_out.at[FG], 10)
-    save(w.at[FU], w_out.at[FU], 11)
-    save(ffn_in, ffn_in_out, 12)
-    save(hidden, hidden_out, 13)
-    for i in reversed(range(len(place.masks) - 1)):
-        weights.forward(FD, i)
-    weights.finish(FD)
-    save(w.at[FD], w_out.at[FD], 14)
-    size = gate_hidden.shape[1]
-
     def feed_back(r, i):
         back = dot_nn(cot_all[r, :], w[FD])
         gate = gate_hidden[r, :]
@@ -584,8 +510,122 @@
         grads[r, :size] = (back * up_hidden[r, :] * slope).astype(BF)
         grads[r, size:] = (back * value).astype(BF)
 
-    over(rows_all, tile, feed_back)
-    save(grads, grads_out, 15)
+    def small_step():
+        pltpu.make_async_copy(x_hbm, x_ref, out_sem.at[16]).wait()
+        for copy in small:
+            copy.wait()
+        spread_small(place, small_ref, small_in, params_ref, group_ref, cum_row_ref, block)
+
+    def norm_step():
+        over(tokens, 16, first_norm)
+
+    def cot_start():
+        pltpu.make_async_copy(cot_hbm, ag_cot.slot(0), out_sem.at[17]).wait()
+        ag_cot.start()
+
+    def chips(ag):
+        lax.fori_loop(0, 4, lambda b, carry: (ag.chip(2 * b), carry)[1], 0)
+
+    def qk_step():
+        chips(ag_normed)
+        weights.finish(QK)
+        over(rows_all, tile, make_qk)
+        save(normed_all, normed_out, 0)
+        save(w.at[QK], w_out.at[QK], 1)
+        save(params_ref, params_out, 18)
+        save(group_ref, group_out, 19)
+        save(cum_row_ref, cumul_out, 20)
+
+    def v_step():
+        weights.finish(V)
+        over(rows_all, tile, make_v)
+        over(rows_all, tile, retention)
+        save(w.at[V], w_out.at[V], 2)
+        save(qkv, qkv_out, 3)
+        save(mixed, mixed_out, 4)
+
+    def g_step():
+        weights.finish(G)
+        over(rows_all, tile, gating)
+        save(w.at[G], w_out.at[G], 5)
+        save(gate_in, gate_out, 6)
+
+    def o_step():
+        weights.finish(O)
+        lax.fori_loop(0, 4, branch_part, 0)
+        save(w.at[O], w_out.at[O], 7)
+
+    def second_step():
+        branch.wait_own()
+        over(tokens, 16, second_norm)
+        save(middle, middle_out, 9)
+
+    def feed_step(b):
+        if b == 0:
+            weights.finish(FG)
+            weights.finish(FU)
+            save(w.at[FG], w_out.at[FG], 10)
+            save(w.at[FU], w_out.at[FU], 11)
+
+        def one(i, carry):
+            ag_two.chip(2 * i)
+            feed(i)
+            return carry
+
+        lax.fori_loop(b, b + 1, one, 0)
+
+    def last_step():
+        save(ffn_in, ffn_in_out, 12)
+        save(hidden, hidden_out, 13)
+        chips(ag_cot)
+        save(cot_all, cot_out, 8)
+        weights.finish(FD)
+        save(w.at[FD], w_out.at[FD], 14)
+        over(rows_all, tile, feed_back)
+        save(grads, grads_out, 15)
+
+    steps = {
+        "small": small_step,
+        "ln": norm_step,
+        "ns": ag_normed.start,
+        "nfz": ag_normed.from_z,
+        "nfy": ag_normed.from_y,
+        "nfzy": ag_normed.from_zy,
+        "ks": cot_start,
+        "kfz": ag_cot.from_z,
+        "kfy": ag_cot.from_y,
+        "kfzy": ag_cot.from_zy,
+        "ts": ag_two.start,
+        "tfz": ag_two.from_z,
+        "tfy": ag_two.from_y,
+        "tfzy": ag_two.from_zy,
+        "qk": qk_step,
+        "v": v_step,
+        "g": g_step,
+        "o": o_step,
+        "p3": lambda: branch.pass_on(3),
+        "p1": lambda: branch.pass_on(1),
+        "p2": lambda: branch.pass_on(2),
+        "ln2": second_step,
+        "feedA": lambda: feed_step(0),
+        "feedB": lambda: feed_step(1),
+        "feedC": lambda: feed_step(2),
+        "feedD": lambda: feed_step(3),
+        "back": last_step,
+    }
+    for name in FORWARD:
+        if name[1:].isdigit():
+            g = int(name[1])
+            if name[0] == "x":
+                weights.own(g)
+            elif name[0] == "s":
+                weights.start(g, int(name[2]) - 1)
+            elif name[0] == "f":
+                weights.forward(g, int(name[2]) - 1)
+            else:
+                steps[name]()
+        else:
+            steps[name]()
     for copy in outs:
         copy.wait()
     for g in range(GROUPS):
@@ -765,12 +805,15 @@
             self.keep.at[g, self.rows(self.place.z), :], self.own_out.at[g], self.own_sem.at[g]
         )
 
-    def pass_on(self, g, ring):
-        for position, i, peer in self.targets:
+    def step(self, g, ring, third):
+        if third == 0:
+            self.add(g, ring, self.place.z)
+            self.own_copy(g).start()
+            return
+        count = len(self.targets)
+        for position, i, peer in self.targets[(3 - third) * count // 3 : (4 - third) * count // 3]:
             self.add(g, ring, position)
             self.z_copy(g, position, i, peer).start()
-        self.add(g, ring, self.place.z)
-        self.own_copy(g).start()
 
     def finish(self, g):
         self.own_copy(g).wait()
@@ -876,7 +919,7 @@
     result = ffn_in.at[:tokens, :]
     weighted = ffn_in.at[tokens : tokens + length, :length]
     score_back = ffn_in.at[tokens : tokens + length, length : 2 * length]
-    ring = {FD: 0, FG: 1, FU: 2, O: 3, QK: 0, V: 1, G: 2}
+    ring = {FD: 0, FG: 1, FU: 2, O: 3, G: 0, QK: 1, V: 2}
 
     def load(src, dst, index):
         copy = pltpu.make_async_copy(src, dst, load_sem.at[index])
@@ -906,12 +949,13 @@
     sums[...] = jnp.zeros_like(sums)
     group_sum[...] = jnp.zeros_like(group_sum)
     entry_barrier(place, True)
-    in_cot.wait()
-    in_hidden.wait()
-    dw.upper(FD, ring[FD], tokens_a, slim, 2 * cols, step)
-    in_grads.wait()
-    in_fg.wait()
-    in_fu.wait()
+    waited = []
+
+    def ready(*copies):
+        for copy in copies:
+            if not any(copy is other for other in waited):
+                waited.append(copy)
+                copy.wait()
 
     def rows_of(i):
         return 3 - i, pl.ds(pl.multiple_of((3 - i) * tile, tile), tile)
@@ -920,21 +964,6 @@
         b, r = rows_of(i)
         rs_two.part(b, dot_nt(slim[r, :cols], w[0]) + dot_nt(slim[r, cols : 2 * cols], w[1]))
         return carry
-
-    lax.fori_loop(0, 4, two_part, 0)
-    in_fd = load(w_ref.at[FD], w.at[0], 1)
-    in_qk = load(w_ref.at[QK], w.at[1], 2)
-    rs_two.pass_on(3)
-    rs_two.pass_on(1)
-    in_ffn.wait()
-    dw.upper(FG, ring[FG], ffn_in, slim, 0, step)
-    dw.upper(FU, ring[FU], ffn_in, slim, cols, step)
-    dw.lower(FD, tokens_a, slim, 2 * cols, step)
-    dw.lower(FG, ffn_in, slim, 0, step)
-    rs_two.pass_on(2)
-    dw.lower(FU, ffn_in, slim, cols, step)
-    in_mixed.wait()
-    in_gate.wait()
 
     def gating(r, i):
         value = mixed[r, :]
@@ -944,10 +973,6 @@
         flat = center * lax.rsqrt(jnp.maximum(spread, GROUP_FLOOR)) * group_ref[...]
         gated[r, :] = (flat * (gate * lax.logistic(gate))).astype(BF)
 
-    over(rows_all, tokens, gating)
-    in_middle.wait()
-    rs_two.wait_own()
-
     def second_back(r, i):
         back, gain_sum, bias_sum = norm_back(middle[r, :], rs_two.own(r), params_ref[1:2, :])
         total = tokens_a[r, :].astype(F32) + back
@@ -956,26 +981,10 @@
         sums[1:2, :] += gain_sum
         sums[3:4, :] += bias_sum
 
-    over(tokens, 16, second_back)
-    ag.start()
-    in_normed = load(normed_ref, tokens_a, 3)
-    rs_two.sent()
-    in_fd.wait()
-    dw.pass_on(FD, ring[FD])
-
     def out_part(i, carry):
         b, r = rows_of(i)
         rs_out.part(b, dot_nt(slim[r, 2 * cols :], w[0]))
         return carry
-
-    lax.fori_loop(0, 4, out_part, 0)
-    in_v = load(w_ref.at[V], w.at[0], 1)
-    ag.from_z()
-    ag.from_y()
-    rs_out.pass_on(3)
-    rs_out.pass_on(1)
-    in_o.wait()
-    in_qkv.wait()
 
     def gating_back(b):
         r = pl.ds(pl.multiple_of(b * tile, tile), tile)
@@ -1021,47 +1030,8 @@
         slim[seq, cols : 2 * cols] = dot_tn(weighted[...], slim[seq, cols : 2 * cols]).astype(BF)
 
 
-    def gating_chips(b, carry):
-        ag.chip(2 * b)
-        gating_back(b)
-        return carry
-
-    lax.fori_loop(0, 2, gating_chips, 0)
-    dw.pass_on(FG, ring[FG])
-    ag.from_zy()
-    lax.fori_loop(2, 4, gating_chips, 0)
-    in_g = load(w_ref.at[G], w.at[2], 9)
-    dw.upper(O, ring[O], branch_all, gated, 0, step)
-
-    def sequences(s, carry):
-        sequence_back(s)
-        return carry
-
-    lax.fori_loop(0, 2, sequences, 0)
-    in_normed.wait()
-    dw.x_sent(FD, ring[FD])
-    dw.upper(QK, ring[QK], tokens_a, slim, 0, step)
-    dw.x_sent(FG, ring[FG])
-    dw.upper(V, ring[V], tokens_a, slim, cols, step)
-    dw.lower(O, branch_all, gated, 0, step)
-    rs_out.pass_on(2)
-    dw.pass_on(FU, ring[FU])
-    dw.x_sent(FU, ring[FU])
-    dw.upper(G, ring[G], tokens_a, slim, 2 * cols, step)
-    dw.lower(QK, tokens_a, slim, 0, step)
-    dw.lower(V, tokens_a, slim, cols, step)
-    dw.lower(G, tokens_a, slim, 2 * cols, step)
-    rs_out.wait_own()
-
     def finish_out(r, i):
         result[r, :] = (middle[r, :] + rs_out.own(r)).astype(BF)
-
-    over(tokens, 16, finish_out)
-    out_layer = load(result, layer_out, 4)
-    rs_out.sent()
-    in_qk.wait()
-    in_v.wait()
-    in_g.wait()
 
     def one_part(i, carry):
         b, r = rows_of(i)
@@ -1069,63 +1039,174 @@
         rs_one.part(b, total + dot_nt(slim[r, 2 * cols :], w[2]))
         return carry
 
-    lax.fori_loop(0, 4, one_part, 0)
-    rs_one.pass_on(3)
-    rs_one.pass_on(1)
-    dw.pass_on(O, ring[O])
-    rs_one.pass_on(2)
-    dw.pass_on(QK, ring[QK])
-    out_layer.wait()
-    rs_one.wait_own()
-
-    pltpu.make_async_copy(x_hbm, x_ref, load_sem.at[11]).wait()
-
     def first_back(r, i):
         back, gain_sum, bias_sum = norm_back(x_ref[r, :].astype(F32), rs_one.own(r), params_ref[0:1, :])
         result[r, :] = (grad_middle[r, :] + back).astype(BF)
         sums[0:1, :] += gain_sum
         sums[2:3, :] += bias_sum
 
-    over(tokens, 16, first_back)
-    out_grad = load(result, input_grad_out, 4)
-
-    def sum_copy(k, peer):
+    def sum_copy(k):
+        peer = (place.c_peer(), place.y_peer())[k]
         return remote(sums, sums_in.at[k], sum_send.at[k], sum_recv.at[k], peer)
 
-    for k, peer in enumerate((place.c_peer(), place.y_peer())):
-        sum_copy(k, peer).start()
-        sum_copy(k, peer).wait()
-        sums[...] += sums_in[k]
-    pieces = cols // block
-    for p in range(n_dp):
-        payload[p, 0:4, :] = sums[0:4, p * block : (p + 1) * block]
-        for k in range(pieces):
-            payload[p, 4 + k : 5 + k, :] = group_sum[0:1, k * block : (k + 1) * block]
     pay = []
     for j, (bits, above, flips) in enumerate(place.pairs):
         position = (1 - place.z if flips else place.z) + above
-        copy = remote(payload.at[position], payload_in.at[j], pay_send.at[j], pay_recv.at[j], place.peer(bits))
-        copy.start()
-        pay.append(copy)
-    dw.pass_on(V, ring[V])
-    for copy in pay:
-        copy.wait()
-    mine = payload[place.z]
-    other = jnp.zeros_like(mine)
-    for j, (bits, above, flips) in enumerate(place.pairs):
-        if flips:
-            other = other + payload_in[j]
+        pay.append(remote(payload.at[position], payload_in.at[j], pay_send.at[j], pay_recv.at[j], place.peer(bits)))
+
+    later = {}
+    operands = {
+        FD: (tokens_a, 2 * cols),
+        FG: (ffn_in, 0),
+        FU: (ffn_in, cols),
+        O: (branch_all, None),
+        QK: (tokens_a, 0),
+        V: (tokens_a, cols),
+        G: (tokens_a, 2 * cols),
+    }
+
+    def operands_of(g):
+        ready(*{FD: (in_cot, in_hidden), FG: (in_ffn, in_grads), FU: (in_ffn, in_grads), O: ()}.get(g, (later.get(3),)))
+        left, col = operands[g]
+        return (left, gated, 0, step) if col is None else (left, slim, col, step)
+
+    def two_step():
+        ready(in_grads, in_fg, in_fu)
+        lax.fori_loop(0, 4, two_part, 0)
+        later[FD] = load(w_ref.at[FD], w.at[0], 1)
+        later[QK] = load(w_ref.at[QK], w.at[1], 2)
+
+    def gating_step():
+        ready(in_mixed, in_gate)
+        over(rows_all, tokens, gating)
+
+    def second_step():
+        ready(in_middle)
+        rs_two.wait_own()
+        over(tokens, 16, second_back)
+        later[3] = load(normed_ref, tokens_a, 3)
+
+    def out_step():
+        rs_two.sent()
+        ready(later[FD])
+        lax.fori_loop(0, 4, out_part, 0)
+        later[V] = load(w_ref.at[V], w.at[0], 1)
+
+    def chip_step(first):
+        ready(in_o, in_qkv)
+
+        def chip(b, carry):
+            ag.chip(2 * b)
+            gating_back(b)
+            return carry
+
+        lax.fori_loop(first, first + 2, chip, 0)
+        if first:
+            later[G] = load(w_ref.at[G], w.at[2], 9)
+
+    def sequence_step(s):
+        lax.fori_loop(s, s + 1, lambda i, carry: (sequence_back(i), carry)[1], 0)
+
+    def out_finish():
+        rs_out.wait_own()
+        over(tokens, 16, finish_out)
+        later["layer"] = load(result, layer_out, 4)
+
+    def one_step():
+        rs_out.sent()
+        ready(later[QK], later[V], later[G])
+        lax.fori_loop(0, 4, one_part, 0)
+
+    def first_step():
+        pltpu.make_async_copy(x_hbm, x_ref, load_sem.at[11]).wait()
+        ready(later["layer"])
+        rs_one.wait_own()
+        over(tokens, 16, first_back)
+        later["grad"] = load(result, input_grad_out, 4)
+
+    def sum_cores():
+        sum_copy(0).start()
+
+    def sum_chips():
+        sum_copy(0).wait()
+        sums[...] += sums_in[0]
+        sum_copy(1).start()
+
+    def pay_start():
+        sum_copy(1).wait()
+        sums[...] += sums_in[1]
+        for p in range(n_dp):
+            payload[p, 0:4, :] = sums[0:4, p * block : (p + 1) * block]
+            for k in range(cols // block):
+                payload[p, 4 + k : 5 + k, :] = group_sum[0:1, k * block : (k + 1) * block]
+        for copy in pay:
+            copy.start()
+
+    def pay_finish():
+        for copy in pay:
+            copy.wait()
+        mine = payload[place.z]
+        other = jnp.zeros_like(mine)
+        for j, (bits, above, flips) in enumerate(place.pairs):
+            if flips:
+                other = other + payload_in[j]
+            else:
+                mine = mine + payload_in[j]
+        sums_out[0] = mine
+        sums_out[1] = other
+
+    before = {G: FD, QK: FG, V: FU}
+
+    def upper(g):
+        if g in before:
+            dw.x_sent(before[g], ring[before[g]])
+        dw.upper(g, ring[g], *operands_of(g))
+
+    steps = {
+        "two": two_step,
+        "a3": lambda: rs_two.pass_on(3),
+        "a1": lambda: rs_two.pass_on(1),
+        "a2": lambda: rs_two.pass_on(2),
+        "gat": gating_step,
+        "lnb": second_step,
+        "bs": ag.start,
+        "bfz": ag.from_z,
+        "bfy": ag.from_y,
+        "bfzy": ag.from_zy,
+        "out": out_step,
+        "o3": lambda: rs_out.pass_on(3),
+        "o1": lambda: rs_out.pass_on(1),
+        "o2": lambda: rs_out.pass_on(2),
+        "gbA": lambda: chip_step(0),
+        "gbB": lambda: chip_step(2),
+        "seq0": lambda: sequence_step(0),
+        "seq1": lambda: sequence_step(1),
+        "outf": out_finish,
+        "one": one_step,
+        "b3": lambda: rs_one.pass_on(3),
+        "b1": lambda: rs_one.pass_on(1),
+        "b2": lambda: rs_one.pass_on(2),
+        "lna": first_step,
+        "sc": sum_cores,
+        "sy": sum_chips,
+        "pay": pay_start,
+        "payw": pay_finish,
+    }
+    for name in BACKWARD:
+        if name in steps:
+            steps[name]()
+        elif name[0] == "u":
+            upper(int(name[1]))
+        elif name[0] == "l":
+            dw.lower(int(name[1]), *operands_of(int(name[1])))
         else:
-            mine = mine + payload_in[j]
-    sums_out[0] = mine
-    sums_out[1] = other
-    dw.pass_on(G, ring[G])
-    out_grad.wait()
-    for g in (O, QK, V, G):
+            dw.step(int(name[1]), ring[int(name[1])], int(name[2]))
+    ready(later["grad"])
+    for g in (O, G, QK, V):
         dw.x_sent(g, ring[g])
     ag.sent()
     rs_one.sent()
-    for g in (FD, FG, FU, O, QK, V, G):
+    for g in (FD, FG, FU, O, G, QK, V):
         dw.finish(g)
 
 

time: 460 us -> 415 us (0.902)
  Pallas kernels: 448 us -> 403 us
    pallas_call x1, Pallas kernels: 220 us -> 196 us  [forward_call(): pl.pallas_call(functools.partial(forward_kernel, n_dp), out_shape=outs, i...]
    pallas_call x1, Pallas kernels: 220 us -> 199 us  [backward_call(): pl.pallas_call(functools.partial(backward_kernel, n_dp), out_shape=outs,...]
where the time goes in v1:
time: 415 us; the launch traced here: 414 us
  Pallas kernels  403 us (97%)
  local copies, waits for them, and re-layouts  6.86 us (2%)
    pallas_call x1, Pallas kernels, backward_call(): pl.pallas_call(functools.partial(backward_kernel, n_dp), out_shape=outs,...  199 us
    pallas_call x1, Pallas kernels, forward_call(): pl.pallas_call(functools.partial(forward_kernel, n_dp), out_shape=outs, i...  196 us

profile of v1, /device:TPU:0, one launch (start us, length us, event | category | flops | bytes accessed | tf_op | source)
XLA Modules:
  0.0 414.3 jit_solution(672211280819231089)
XLA Ops:
  0.7 0.7 convert_element_type.11
  1.4 0.7 convert_element_type.12
  2.1 0.7 reshape.71
  2.8 0.6 reduce-window.6
  3.4 0.2 slice_reduce_fusion
  3.5 0.2 reduce-window.9
  3.7 0.1 broadcast_add_fusion
  3.8 0.1 maximum_select_fusion
  3.9 0.1 maximum_select_fusion.1
  4.0 0.7 tile.4
  4.7 0.1 tile.10
  4.8 0.6 select_maximum_fusion.small_ref
  5.4 2.0 copy.29
  7.4 2.0 copy.30
  9.5 1.1 fusion.1
  10.6 0.9 pad_maximum_fusion.s_qk
  11.5 195.7 %shard_map.237 = (bf16[7,2048,512]{2,1,0:T(8,128)(2,1)}, bf16[1024,2048]{1,0:T(8,128)(2,1)}, bf16[1024,1024]{1,0:T(8,128)(2,1)}, f32[1024,512]{1,0:T(8,128)}, f3...) custom-call(bf16[128,2048]{1,0:T(8,128)(2,1)} %x_hbm.3, ...), custom_call_target="tpu_custom_call" | custom-call | tf_op jit(solution)/shard_map/pallas_call | solution.py:715
  207.2 198.9 %shard_map.238 = (bf16[128,2048]{1,0:T(8,128)(2,1)}, bf16[128,2048]{1,0:T(8,128)(2,1)}, bf16[7,256,512]{2,1,0:T(8,128)(2,1)}, bf16[7,3,256,512]{3,2,1,0:T(8,128)(2,1)}, f32[2,8,256]{2,1,0:T(8,128)}) custom-call(bf16[128,2048]{1,0:T(8,128)(2,1)} %x_hbm.3, f32[8,2048]{1,0:T(8,128)} %get-tuple-element.31.params_ref, f32[1,512]{1,0:T(1,128)} %get-tuple-element.32.group_ref, ...), custom_call_target="tpu_custom_call" | custom-call | tf_op jit(solution)/shard_map/pallas_call | solution.py:1275
  406.1 8.0 %shard_map.239 = (bf16[128,2048]{1,0:T(8,128)(2,1)}, bf16[128,2048]{1,0:T(8,128)(2,1)}, f32[256,512]{1,0:T(8,128)}, f32[256,512]{1,0:T(8,128)}, f32[256,1024]{1,...) custom-call(bf16[7,256,512]{2,1,0:T(8,128)(2,1)} %get-tuple-element., ...), custom_call_target="tpu_custom_call" | custom-call | tf_op jit(solution)/shard_map/pallas_call | solution.py:1418
  (8 shorter events, 0.1 us)

commit v2 on v1

--- a/solution.py
+++ b/solution.py
@@ -26,11 +26,11 @@
     "feedA", "tfy", "s62", "tfz", "feedB", "f63", "f62", "tfzy", "feedC", "feedD", "back",
 )
 BACKWARD = (
-    "u6", "two", "a3", "l6", "s63", "a1", "a2", "l4", "u4", "lnb", "bs", "u5", "s60", "gat", "l5", "s43", "out",
-    "bfz", "s53", "s61", "bfy", "gbA", "s40", "bfzy", "s52", "s41", "gbB", "u3", "seq0", "seq1", "o3", "u2", "l0",
-    "s42", "s51", "s62", "l2", "u0", "s50", "o1", "l3", "o2", "s32", "u1", "s21", "s23", "s33", "s31", "outf",
-    "one", "s30", "l1", "b3", "b1", "s22", "b2", "s02", "s13", "s01", "lna", "s00", "s10", "s11", "s03", "s20",
-    "sc", "sy", "pay", "s12", "payw",
+    "u6", "two", "a3", "l6", "s63", "u4", "a1", "a2", "l4", "s43", "lnb", "bs", "gat", "out", "o3", "l5", "s42",
+    "bfy", "u5", "s62", "s41", "bfz", "gbA", "s40", "o1", "o2", "bfzy", "s53", "s52", "gbB", "u3", "seq0", "l3",
+    "s60", "s61", "seq1", "outf", "one", "s51", "s33", "u1", "u2", "s32", "b3", "b2", "u0", "s30", "l1", "l0",
+    "s13", "s12", "b1", "s50", "lna", "s11", "l2", "sc", "s22", "s21", "sy", "s20", "pay", "s31", "s10", "s23",
+    "s01", "s03", "s02", "payw", "s00",
 )
 
 
@@ -100,12 +100,19 @@
         return near + [self.peer(bits) for bits, _, _ in self.masks]
 
 
+def greet(place, far):
+    barrier = pltpu.get_barrier_semaphore()
+    for peer in place.everyone(far):
+        pl.semaphore_signal(barrier, inc=1, device_id=peer, device_id_type=MESH)
+
+
+def met(place, far):
+    pl.semaphore_wait(pltpu.get_barrier_semaphore(), len(place.everyone(far)))
+
+
 def entry_barrier(place, far=False):
-    barrier = pltpu.get_barrier_semaphore()
-    peers = place.everyone(far)
-    for peer in peers:
-        pl.semaphore_signal(barrier, inc=1, device_id=peer, device_id_type=MESH)
-    pl.semaphore_wait(barrier, len(peers))
+    greet(place, far)
+    met(place, far)
 
 
 def column_copies(place, src, dst, sem, block, back=False):
@@ -130,26 +137,26 @@
     def __init__(self, place, sources, full, sems):
         self.place, self.sources, self.full = place, sources, full
         self.z_send, self.z_recv, self.x_send, self.x_recv, self.local = sems
-        self.block = sources[0].shape[0]
-        self.cols = sources[0].shape[1] // 2
+        self.block = sources[-1].shape[0]
+        self.cols = sources[-1].shape[1] // 2
         self.half = place.n_dp // 2
 
     def rows(self, position, count=1):
         return pl.ds(pl.multiple_of(position * self.block, self.block), count * self.block)
 
-    def source(self, g, half):
-        return self.sources[g].at[:, pl.ds(pl.multiple_of(half * self.cols, self.cols), self.cols)]
+    def pairs(self, g, half, position):
+        parts = self.sources[g] if isinstance(self.sources[g], tuple) else (self.sources[g],)
+        count = self.cols // len(parts)
+        for k, part in enumerate(parts):
+            columns = pl.ds(pl.multiple_of(half * count, count), count)
+            yield part.at[:, columns], self.full.at[g, self.rows(position), k * count : (k + 1) * count]
 
     def own(self, g):
         z = self.place.z
-        pltpu.make_async_copy(self.source(g, z), self.full.at[g, self.rows(z), :], self.local.at[g]).start()
-        remote(
-            self.source(g, z),
-            self.full.at[g, self.rows(z + self.half), :],
-            self.x_send.at[g],
-            self.x_recv.at[g],
-            self.place.x_peer(),
-        ).start()
+        for src, dst in self.pairs(g, z, z):
+            pltpu.make_async_copy(src, dst, self.local.at[g]).start()
+        for src, dst in self.pairs(g, z, z + self.half):
+            remote(src, dst, self.x_send.at[g], self.x_recv.at[g], self.place.x_peer()).start()
 
     def some(self, third):
         count = len(self.place.masks)
@@ -159,13 +166,8 @@
         z = self.place.z
         for i in self.some(third):
             bits, above, flips = self.place.masks[i]
-            remote(
-                self.source(g, 1 - z if flips else z),
-                self.full.at[g, self.rows(z + above), :],
-                self.z_send.at[g],
-                self.z_recv.at[g, i],
-                self.place.peer(bits),
-            ).start()
+            for src, dst in self.pairs(g, 1 - z if flips else z, z + above):
+                remote(src, dst, self.z_send.at[g], self.z_recv.at[g, i], self.place.peer(bits)).start()
 
     def forward(self, g, third):
         for i in self.some(third):
@@ -183,7 +185,8 @@
 
     def finish(self, g):
         z = self.place.z
-        pltpu.make_async_copy(self.source(g, z), self.full.at[g, self.rows(z), :], self.local.at[g]).wait()
+        here = self.full.at[g, self.rows(z), :]
+        pltpu.make_async_copy(here, here, self.local.at[g]).wait()
         there = self.full.at[g, self.rows(self.half, self.half), :]
         remote(there, there, self.x_send.at[g], self.x_recv.at[g], self.place.x_peer()).wait_recv()
 
@@ -322,6 +325,36 @@
     return jnp.where(causal, jnp.exp(jnp.where(causal, cumul_cols - cumul_rows, 0.0)), 0.0)
 
 
+def pack_small(place, small, gains, biases, group, decay, tokens):
+    block = small.shape[1]
+    wide = place.n_dp * group.shape[1]
+    length = decay.shape[1]
+    small[...] = jnp.zeros_like(small)
+    small[0:2, :] = gains[...].astype(F32)
+    small[2:4, :] = biases[...].astype(F32)
+    lane = lax.broadcasted_iota(jnp.int32, (2, wide), 1)
+    tiled = jnp.concatenate([group[...].astype(F32)] * place.n_dp, axis=1)
+    spread = jnp.where(lane // group.shape[1] == place.d, tiled, 0.0)
+    at = 4
+    for h in range(2):
+        for k in range(wide // block):
+            small[at : at + 1, :] = spread[h : h + 1, k * block : (k + 1) * block]
+            at += 1
+    total = decay[...]
+    lane = lax.broadcasted_iota(jnp.int32, total.shape, 1)
+    shift = 1
+    while shift < length:
+        total = total + jnp.where(lane >= shift, pltpu.roll(total, shift, 1), 0.0)
+        shift *= 2
+    for bit in (1, 2):
+        pieces = [total[:, (j ^ bit) * tokens : ((j ^ bit) + 1) * tokens] for j in range(length // tokens)]
+        total = jnp.where((place.t // bit) % 2 == 1, jnp.concatenate(pieces, axis=1), total)
+    for h in range(2):
+        for k in range(length // block):
+            small[at : at + 1, :] = total[h : h + 1, k * block : (k + 1) * block]
+            at += 1
+
+
 def spread_small(place, own, others, params, group, cumul, block):
     pieces = group.shape[1] // block
     steps = cumul.shape[1] // block
@@ -357,8 +390,12 @@
     n_dp,
     x_hbm,
     cot_hbm,
-    small_ref,
-    s_qk,
+    gains_ref,
+    biases_ref,
+    group_gain_ref,
+    decay_ref,
+    s_q,
+    s_k,
     s_v,
     s_g,
     s_o,
@@ -378,7 +415,10 @@
     params_out,
     group_out,
     cumul_out,
+    small_ref,
     small_in,
+    turned,
+    natural,
     params_ref,
     group_ref,
     cum_row_ref,
@@ -424,7 +464,7 @@
     head_k = qkv.shape[1] // 4
     scale = 1.0 / math.sqrt(head_k)
     tile = 2 * tokens
-    weights = Weights(place, [s_qk, s_v, s_g, s_o, s_fg, s_fu, s_fd], w, (z_send, z_recv, x_send, x_recv, w_local))
+    weights = Weights(place, [(s_q, s_k), s_v, s_g, turned.at[0], s_fg, s_fu, turned.at[1]], w, (z_send, z_recv, x_send, x_recv, w_local))
     ag_normed = Gather(place, normed_all, ag_send.at[0], ag_recv.at[0])
     ag_cot = Gather(place, cot_all, ag_send.at[1], ag_recv.at[1])
     ag_two = Gather(place, ffn_in, ag_send.at[2], ag_recv.at[2])
@@ -447,7 +487,20 @@
         copy.start()
     for copy in column_copies(place, cot_hbm, ag_cot.slot(0), out_sem.at[17], block):
         copy.start()
-    entry_barrier(place, True)
+    flat = [
+        pltpu.make_async_copy(s_o, natural.at[0], out_sem.at[21]),
+        pltpu.make_async_copy(s_fd, natural.at[1], out_sem.at[22]),
+    ]
+    for copy in flat:
+        copy.start()
+    greet(place, True)
+    pack_small(place, small_ref, gains_ref, biases_ref, group_gain_ref, decay_ref, tokens)
+    for k, copy in enumerate(flat):
+        copy.wait()
+        cols = w.shape[2]
+        for j in range(2):
+            turned[k, :, j * cols : (j + 1) * cols] = natural[k, j * cols : (j + 1) * cols, :].T
+    met(place, True)
     small = []
     for j, (bits, above, flips) in enumerate(place.pairs):
         copy = remote(small_ref, small_in.at[j], small_send.at[j], small_recv.at[j], place.peer(bits))
@@ -649,11 +702,13 @@
     return 0.5 * v * (1.0 + inside), slope
 
 
-def forward_call(n_dp, x, cot, small, sources):
+def forward_call(n_dp, x, cot, smalls, sources):
     tokens, width = x.shape
     length = 4 * tokens
+    block = width // n_dp
     rows_all = 8 * tokens
-    cols = sources[0].shape[1] // 2
+    cols = sources[2].shape[1] // 2
+    small_rows = -(-(4 + 2 * (cols + length) // block) // 8) * 8
     masks = n_dp // 2 - 1
     vmem, hbm = pl.BlockSpec(memory_space=pltpu.VMEM), pl.BlockSpec(memory_space=pl.ANY)
     shape = jax.ShapeDtypeStruct
@@ -674,7 +729,10 @@
     )
     dma = pltpu.SemaphoreType.DMA
     scratch = [
-        pltpu.VMEM((n_dp - 1, *small.shape), F32),
+        pltpu.VMEM((small_rows, block), F32),
+        pltpu.VMEM((n_dp - 1, small_rows, block), F32),
+        pltpu.VMEM((2, block, 2 * cols), BF),
+        pltpu.VMEM((2, 2 * cols, block), BF),
         pltpu.VMEM((8, width), F32),
         pltpu.VMEM((1, cols), F32),
         pltpu.VMEM((2, length), F32),
@@ -708,20 +766,20 @@
         dma((4,)),
         dma((3,)),
         dma((3,)),
-        dma((21,)),
+        dma((23,)),
         dma((n_dp - 1,)),
         dma((n_dp - 1,)),
     ]
     return pl.pallas_call(
         functools.partial(forward_kernel, n_dp),
         out_shape=outs,
-        in_specs=[hbm, hbm, vmem] + [hbm] * GROUPS,
+        in_specs=[hbm, hbm] + [vmem] * 4 + [hbm] * len(sources),
         out_specs=(hbm,) * len(outs),
         scratch_shapes=scratch,
         compiler_params=pltpu.CompilerParams(
             collective_id=1, has_side_effects=True, vmem_limit_bytes=64_000_000
         ),
-    )(x, cot, small, *sources)
+    )(x, cot, *smalls, *sources)
 
 
 class Reduce:
@@ -1456,7 +1514,6 @@
     d, t = place.d, place.t
     tokens, width = inputs.shape
     block = width // n_dp
-    head_v = value_weight.shape[1] // 2
 
     def position_of(q):
         out = (q // PAIR) & 1
@@ -1471,36 +1528,19 @@
             [lax.dynamic_slice_in_dim(value, index(p) * block, block, 1) for p in range(n_dp)], axis=1
         )
 
-    def half(value, which, axis):
-        size = value.shape[axis] // 2
-        return lax.dynamic_slice_in_dim(value, which * size, size, axis)
-
-    cumul = jnp.cumsum(log_decay, axis=1).reshape(2, n_tensor, tokens)
-    for bit in (1, 2):
-        swapped = jnp.concatenate([cumul[:, j ^ bit : (j ^ bit) + 1] for j in range(n_tensor)], axis=1)
-        cumul = jnp.where((t // bit) % 2 == 1, swapped, cumul)
-    spread = jnp.tile(group_gain.astype(F32), (1, n_dp))
-    spread = jnp.where(lax.broadcasted_iota(jnp.int32, spread.shape, 1) // (head_v // n_dp) == d, spread, 0.0)
-    parts = [norm_gains.astype(F32), norm_biases.astype(F32), spread, cumul]
-    small = jnp.concatenate([part.reshape(-1, block) for part in parts], axis=0)
-    small = jnp.pad(small, ((0, -small.shape[0] % 8), (0, 0)))
-
-    def interleaved(first, second):
-        parts = [half(first, 0, 1), half(second, 0, 1), half(first, 1, 1), half(second, 1, 1)]
-        return jnp.concatenate(parts, axis=1)
-
-    sources = [
-        interleaved(query_weight, key_weight),
+    smalls = (norm_gains, norm_biases, group_gain, log_decay)
+    sources = (
+        query_weight,
+        key_weight,
         value_weight,
         gate_weight,
-        out_weight.T,
+        out_weight,
         ffn_gate_weight,
         ffn_up_weight,
-        ffn_down_weight.T,
-    ]
-
+        ffn_down_weight,
+    )
     x, cot = moved(inputs, place.dp_of), moved(cotangent, place.dp_of)
-    *saved, params, group, cumul = forward_call(n_dp, x, cot, small, sources)
+    *saved, params, group, cumul = forward_call(n_dp, x, cot, smalls, sources)
     layer, grad, own, others, sums = backward_call(n_dp, x, params, group, cumul, saved)
     outs = finish_call(n_dp, n_tensor, own, others, layer, grad, sums)
     return (moved(outs[0], position_of), moved(outs[1], position_of), *outs[2:])

time: 415 us -> 401 us (0.966)
  local copies, waits for them, and re-layouts: 6.86 us -> 0 us
where the time goes in v2:
time: 401 us
  Pallas kernels  400 us (100%)
    pallas_call x1, Pallas kernels, backward_call(): pl.pallas_call(functools.partial(backward_kernel, n_dp), out_shape=outs,...  197 us
    pallas_call x1, Pallas kernels, forward_call(): pl.pallas_call(functools.partial(forward_kernel, n_dp), out_shape=outs, i...  195 us

profile of v2, /device:TPU:0, one launch (start us, length us, event | category | flops | bytes accessed | tf_op | source)
XLA Modules:
  0.0 400.6 jit_solution(888921103848168545)
XLA Ops:
  0.6 194.6 %shard_map.237 = (bf16[7,2048,512]{2,1,0:T(8,128)(2,1)}, bf16[1024,2048]{1,0:T(8,128)(2,1)}, bf16[1024,1024]{1,0:T(8,128)(2,1)}, f32[1024,512]{1,0:T(8,128)}, f3...) custom-call(bf16[128,2048]{1,0:T(8,128)(2,1)} %x_hbm.3, ...), custom_call_target="tpu_custom_call" | custom-call | tf_op jit(solution)/shard_map/pallas_call | solution.py:773
  195.3 197.1 %shard_map.238 = (bf16[128,2048]{1,0:T(8,128)(2,1)}, bf16[128,2048]{1,0:T(8,128)(2,1)}, bf16[7,256,512]{2,1,0:T(8,128)(2,1)}, bf16[7,3,256,512]{3,2,1,0:T(8,128)(2,1)}, f32[2,8,256]{2,1,0:T(8,128)}) custom-call(bf16[128,2048]{1,0:T(8,128)(2,1)} %x_hbm.3, f32[8,2048]{1,0:T(8,128)} %get-tuple-element.31.params_ref, f32[1,512]{1,0:T(1,128)} %get-tuple-element.32.group_ref, ...), custom_call_target="tpu_custom_call" | custom-call | tf_op jit(solution)/shard_map/pallas_call | solution.py:1333
  392.4 8.0 %shard_map.239 = (bf16[128,2048]{1,0:T(8,128)(2,1)}, bf16[128,2048]{1,0:T(8,128)(2,1)}, f32[256,512]{1,0:T(8,128)}, f32[256,512]{1,0:T(8,128)}, f32[256,1024]{1,...) custom-call(bf16[7,256,512]{2,1,0:T(8,128)(2,1)} %get-tuple-element., ...), custom_call_target="tpu_custom_call" | custom-call | tf_op jit(solution)/shard_map/pallas_call | solution.py:1476

commit v3 on v2

--- a/solution.py
+++ b/solution.py
@@ -19,18 +19,18 @@
 
 
 FORWARD = (
-    "x2", "x3", "x0", "s01", "s22", "s02", "s21", "s41", "s12", "x1", "f01", "s31", "small", "ln", "f22", "ns",
-    "s03", "f41", "f02", "nfy", "s23", "f12", "x6", "s32", "s13", "f31", "s11", "nfz", "f21", "f03", "f32", "ks",
-    "s33", "s53", "nfzy", "f11", "s43", "s51", "f23", "qk", "f13", "kfz", "f33", "v", "g", "f53", "kfy", "s52",
-    "o", "p3", "f51", "p1", "s61", "x5", "f52", "s42", "p2", "f42", "s63", "kfzy", "x4", "f43", "ln2", "f61", "ts",
-    "feedA", "tfy", "s62", "tfz", "feedB", "f63", "f62", "tfzy", "feedC", "feedD", "back",
+    "s22", "s11", "x1", "small", "s32", "ks", "x4", "x3", "x2", "kfy", "ln", "s02", "ns", "s03", "s01", "s31",
+    "f22", "nfy", "f11", "s13", "f32", "f02", "s33", "s23", "x0", "x6", "f01", "f31", "nfz", "nfzy", "s12", "f03",
+    "s21", "f13", "f23", "kfz", "qk", "s51", "s42", "f12", "s52", "f21", "s41", "f33", "s61", "s63", "v", "g", "o",
+    "p3", "f42", "f41", "f61", "p2", "x5", "kfzy", "f63", "s53", "p1", "p2B", "f51", "s43", "ln2", "f52", "ts",
+    "tfy", "f53", "s62", "f43", "tfz", "tfzB", "f62", "feedA", "feedB", "feedC", "tfzy", "feedD", "back",
 )
 BACKWARD = (
-    "u6", "two", "a3", "l6", "s63", "u4", "a1", "a2", "l4", "s43", "lnb", "bs", "gat", "out", "o3", "l5", "s42",
-    "bfy", "u5", "s62", "s41", "bfz", "gbA", "s40", "o1", "o2", "bfzy", "s53", "s52", "gbB", "u3", "seq0", "l3",
-    "s60", "s61", "seq1", "outf", "one", "s51", "s33", "u1", "u2", "s32", "b3", "b2", "u0", "s30", "l1", "l0",
-    "s13", "s12", "b1", "s50", "lna", "s11", "l2", "sc", "s22", "s21", "sy", "s20", "pay", "s31", "s10", "s23",
-    "s01", "s03", "s02", "payw", "s00",
+    "u6", "two", "a3", "a1", "l6", "s63", "l4", "a2", "s62", "u4", "u5", "s43", "lnb", "bs", "bfz", "s42", "s41",
+    "l5", "out", "o3", "s52", "bfy", "s51", "gat", "s40", "gbA", "bfzy", "gbB", "u3", "l2", "u2", "seq0", "s53",
+    "o2", "seq1", "u0", "u1", "l0", "l3", "o1", "s33", "outf", "s32", "s31", "one", "s61", "s23", "s30", "b3",
+    "l1", "b2", "s22", "s02", "b1", "s01", "s21", "s03", "s13", "lna", "s10", "s00", "s20", "sc", "sy", "pay",
+    "s50", "s12", "s60", "s11", "payw",
 )
 
 
@@ -242,6 +242,43 @@
         self.copy(6, 1).wait_send()
 
 
+class HalfGather(Gather):
+    def part(self, source, bit, h):
+        count = self.tokens // 2
+        s = source + bit
+        index = s - 1 if h == 0 else 5 + s // 2
+        src = self.buffer.at[pl.ds(source * self.tokens + h * count, count), :]
+        dst = self.buffer.at[pl.ds(s * self.tokens + h * count, count), :]
+        return remote(src, dst, self.send.at[index], self.recv.at[index], self.peers[bit])
+
+    def start(self):
+        for h in range(2):
+            self.part(0, 4, h).start()
+        self.copy(0, 2).start()
+        self.copy(0, 1).start()
+
+    def from_z(self):
+        self.part(0, 4, 0).wait_recv()
+        self.part(4, 2, 0).start()
+
+    def from_z_rest(self):
+        self.part(0, 4, 1).wait_recv()
+        self.part(4, 2, 1).start()
+        self.copy(4, 1).start()
+
+    def from_zy(self):
+        for h in range(2):
+            self.part(4, 2, h).wait_recv()
+        self.copy(6, 1).start()
+
+    def sent(self):
+        for h in range(2):
+            self.part(0, 4, h).wait_send()
+            self.part(4, 2, h).wait_send()
+        for source, bit in ((0, 2), (0, 1), (4, 1), (2, 1), (6, 1)):
+            self.copy(source, bit).wait_send()
+
+
 class Scatter:
     def __init__(self, place, keep, c_out, c_in, far_out, far_in, sems):
         self.place = place
@@ -305,6 +342,59 @@
             self.c_copy(b).wait_send()
         for b in (3, 2, 1):
             self.far_copy(b).wait_send()
+
+
+class HalfScatter(Scatter):
+    def half_copy(self, b, h):
+        peer = self.place.z_peer() if b == 2 else self.place.y_peer()
+        count = self.tokens // 2
+        rows = pl.ds(h * count, count)
+        index = b - 1 if h == 0 else b + 1
+        return remote(
+            self.far_source(b).at[rows, :],
+            self.far_in.at[b - 1, rows, :],
+            self.far_send.at[index],
+            self.far_recv.at[index],
+            peer,
+        )
+
+    def pass_on(self, b, h=0):
+        if b == 1:
+            super().pass_on(1)
+            return
+        if h == 0:
+            self.c_copy(b).wait_recv()
+        if b == 2:
+            self.half_copy(3, h).wait_recv()
+        step = 16
+        count = self.tokens // 2
+
+        def body(i, carry):
+            r = pl.ds(pl.multiple_of(h * count + i * step, step), step)
+            total = self.keep[b, r, :].astype(F32) + self.c_in[b, r, :].astype(F32)
+            if b == 2:
+                total = total + self.far_in[2, r, :].astype(F32)
+            self.far_source(b)[r, :] = total.astype(BF)
+            return carry
+
+        lax.fori_loop(0, count // step, body, 0)
+        self.half_copy(b, h).start()
+        if b == 3 and h == 0:
+            self.pass_on(3, 1)
+
+    def wait_own(self):
+        self.c_copy(0).wait_recv()
+        self.far_copy(1).wait_recv()
+        for h in range(2):
+            self.half_copy(2, h).wait_recv()
+
+    def sent(self):
+        for b in range(4):
+            self.c_copy(b).wait_send()
+        self.far_copy(1).wait_send()
+        for h in range(2):
+            self.half_copy(3, h).wait_send()
+            self.half_copy(2, h).wait_send()
 
 
 def normalized(value):
@@ -467,8 +557,8 @@
     weights = Weights(place, [(s_q, s_k), s_v, s_g, turned.at[0], s_fg, s_fu, turned.at[1]], w, (z_send, z_recv, x_send, x_recv, w_local))
     ag_normed = Gather(place, normed_all, ag_send.at[0], ag_recv.at[0])
     ag_cot = Gather(place, cot_all, ag_send.at[1], ag_recv.at[1])
-    ag_two = Gather(place, ffn_in, ag_send.at[2], ag_recv.at[2])
-    branch = Scatter(place, keep, c_out, c_in, far_out, far_in, (c_send, c_recv, far_send, far_recv))
+    ag_two = HalfGather(place, ffn_in, ag_send.at[2], ag_recv.at[2])
+    branch = HalfScatter(place, keep, c_out, c_in, far_out, far_in, (c_send, c_recv, far_send, far_recv))
     outs = []
 
     def save(src, dst, index):
@@ -650,6 +740,7 @@
         "kfzy": ag_cot.from_zy,
         "ts": ag_two.start,
         "tfz": ag_two.from_z,
+        "tfzB": ag_two.from_z_rest,
         "tfy": ag_two.from_y,
         "tfzy": ag_two.from_zy,
         "qk": qk_step,
@@ -659,6 +750,7 @@
         "p3": lambda: branch.pass_on(3),
         "p1": lambda: branch.pass_on(1),
         "p2": lambda: branch.pass_on(2),
+        "p2B": lambda: branch.pass_on(2, 1),
         "ln2": second_step,
         "feedA": lambda: feed_step(0),
         "feedB": lambda: feed_step(1),
@@ -760,12 +852,12 @@
         dma((GROUPS,)),
         dma((GROUPS,)),
         dma((GROUPS,)),
-        dma((3, 7)),
-        dma((3, 7)),
+        dma((3, 9)),
+        dma((3, 9)),
         dma((4,)),
         dma((4,)),
-        dma((3,)),
-        dma((3,)),
+        dma((5,)),
+        dma((5,)),
         dma((23,)),
         dma((n_dp - 1,)),
         dma((n_dp - 1,)),

time: 401 us -> 393 us (0.980)
  Pallas kernels: 400 us -> 392 us
    pallas_call x1, Pallas kernels: 197 us -> 191 us  [backward_call(): pl.pallas_call(functools.partial(backward_kernel, n_dp), out_shape=outs,...]
where the time goes in v3:
time: 393 us
  Pallas kernels  392 us (100%)
    pallas_call x1, Pallas kernels, forward_call(): pl.pallas_call(functools.partial(forward_kernel, n_dp), out_shape=outs, i...  193 us
    pallas_call x1, Pallas kernels, backward_call(): pl.pallas_call(functools.partial(backward_kernel, n_dp), out_shape=outs,...  191 us
    pallas_call x1, Pallas kernels, finish_call(): pl.pallas_call(functools.partial(finish_kernel, n_dp), out_shape=outs, in...  7.99 us

profile of v3, /device:TPU:0, one launch (start us, length us, event | category | flops | bytes accessed | tf_op | source)
XLA Modules:
  0.0 392.9 jit_solution(11226904190889346116)
XLA Ops:
  0.6 193.4 %shard_map.237 = (bf16[7,2048,512]{2,1,0:T(8,128)(2,1)}, bf16[1024,2048]{1,0:T(8,128)(2,1)}, bf16[1024,1024]{1,0:T(8,128)(2,1)}, f32[1024,512]{1,0:T(8,128)}, f3...) custom-call(bf16[128,2048]{1,0:T(8,128)(2,1)} %x_hbm.3, ...), custom_call_target="tpu_custom_call" | custom-call | tf_op jit(solution)/shard_map/pallas_call | solution.py:865
  194.1 190.6 %shard_map.238 = (bf16[128,2048]{1,0:T(8,128)(2,1)}, bf16[128,2048]{1,0:T(8,128)(2,1)}, bf16[7,256,512]{2,1,0:T(8,128)(2,1)}, bf16[7,3,256,512]{3,2,1,0:T(8,128)(2,1)}, f32[2,8,256]{2,1,0:T(8,128)}) custom-call(bf16[128,2048]{1,0:T(8,128)(2,1)} %x_hbm.3, f32[8,2048]{1,0:T(8,128)} %get-tuple-element.31.params_ref, f32[1,512]{1,0:T(1,128)} %get-tuple-element.32.group_ref, ...), custom_call_target="tpu_custom_call" | custom-call | tf_op jit(solution)/shard_map/pallas_call | solution.py:1425
  384.7 8.0 %shard_map.239 = (bf16[128,2048]{1,0:T(8,128)(2,1)}, bf16[128,2048]{1,0:T(8,128)(2,1)}, f32[256,512]{1,0:T(8,128)}, f32[256,512]{1,0:T(8,128)}, f32[256,1024]{1,...) custom-call(bf16[7,256,512]{2,1,0:T(8,128)(2,1)} %get-tuple-element., ...), custom_call_target="tpu_custom_call" | custom-call | tf_op jit(solution)/shard_map/pallas_call | solution.py:1568

commit v4 on v3

--- a/solution.py
+++ b/solution.py
@@ -303,7 +303,7 @@
     def far_source(self, b):
         return self.keep.at[b] if self.far_out is None else self.far_out.at[b - 1]
 
-    def rows(self, body, step=16):
+    def rows(self, body, step=64):
         def loop(i, carry):
             body(pl.ds(pl.multiple_of(i * step, step), step))
             return carry
@@ -366,7 +366,7 @@
             self.c_copy(b).wait_recv()
         if b == 2:
             self.half_copy(3, h).wait_recv()
-        step = 16
+        step = 64
         count = self.tokens // 2
 
         def body(i, carry):
@@ -660,7 +660,7 @@
         spread_small(place, small_ref, small_in, params_ref, group_ref, cum_row_ref, block)
 
     def norm_step():
-        over(tokens, 16, first_norm)
+        over(tokens, 32, first_norm)
 
     def cot_start():
         pltpu.make_async_copy(cot_hbm, ag_cot.slot(0), out_sem.at[17]).wait()
@@ -700,7 +700,7 @@
 
     def second_step():
         branch.wait_own()
-        over(tokens, 16, second_norm)
+        over(tokens, 32, second_norm)
         save(middle, middle_out, 9)
 
     def feed_step(b):
@@ -1233,7 +1233,7 @@
     def second_step():
         ready(in_middle)
         rs_two.wait_own()
-        over(tokens, 16, second_back)
+        over(tokens, 32, second_back)
         later[3] = load(normed_ref, tokens_a, 3)
 
     def out_step():
@@ -1271,7 +1271,7 @@
         pltpu.make_async_copy(x_hbm, x_ref, load_sem.at[11]).wait()
         ready(later["layer"])
         rs_one.wait_own()
-        over(tokens, 16, first_back)
+        over(tokens, 32, first_back)
         later["grad"] = load(result, input_grad_out, 4)
 
     def sum_cores():

time: 393 us -> 393 us (level)
  no operation moved by 1% of the time
where the time goes in v4:
time: 393 us; the launch traced here: 392 us
  Pallas kernels  391 us (99%)
    pallas_call x1, Pallas kernels, forward_call(): pl.pallas_call(functools.partial(forward_kernel, n_dp), out_shape=outs, i...  193 us
    pallas_call x1, Pallas kernels, backward_call(): pl.pallas_call(functools.partial(backward_kernel, n_dp), out_shape=outs,...  191 us
    pallas_call x1, Pallas kernels, finish_call(): pl.pallas_call(functools.partial(finish_kernel, n_dp), out_shape=outs, in...  7.99 us

profile of v4, /device:TPU:0, one launch (start us, length us, event | category | flops | bytes accessed | tf_op | source)
XLA Modules:
  0.0 392.2 jit_solution(12152289829637308450)
XLA Ops:
  0.6 192.6 %shard_map.237 = (bf16[7,2048,512]{2,1,0:T(8,128)(2,1)}, bf16[1024,2048]{1,0:T(8,128)(2,1)}, bf16[1024,1024]{1,0:T(8,128)(2,1)}, f32[1024,512]{1,0:T(8,128)}, f3...) custom-call(bf16[128,2048]{1,0:T(8,128)(2,1)} %x_hbm.3, ...), custom_call_target="tpu_custom_call" | custom-call | tf_op jit(solution)/shard_map/pallas_call | solution.py:865
  193.2 190.8 %shard_map.238 = (bf16[128,2048]{1,0:T(8,128)(2,1)}, bf16[128,2048]{1,0:T(8,128)(2,1)}, bf16[7,256,512]{2,1,0:T(8,128)(2,1)}, bf16[7,3,256,512]{3,2,1,0:T(8,128)(2,1)}, f32[2,8,256]{2,1,0:T(8,128)}) custom-call(bf16[128,2048]{1,0:T(8,128)(2,1)} %x_hbm.3, f32[8,2048]{1,0:T(8,128)} %get-tuple-element.31.params_ref, f32[1,512]{1,0:T(1,128)} %get-tuple-element.32.group_ref, ...), custom_call_target="tpu_custom_call" | custom-call | tf_op jit(solution)/shard_map/pallas_call | solution.py:1425
  384.1 8.0 %shard_map.239 = (bf16[128,2048]{1,0:T(8,128)(2,1)}, bf16[128,2048]{1,0:T(8,128)(2,1)}, f32[256,512]{1,0:T(8,128)}, f32[256,512]{1,0:T(8,128)}, f32[256,1024]{1,...) custom-call(bf16[7,256,512]{2,1,0:T(8,128)(2,1)} %get-tuple-element., ...), custom_call_target="tpu_custom_call" | custom-call | tf_op jit(solution)/shard_map/pallas_call | solution.py:1568
